TPU v7x, 64 devices: a 2x2x8 block of a 4x4x8 slice. The times are simulated.
64 devices in a mesh: data: 4 (over x, y), tp: 16 (over z, core).
Axes of the slice: x: 2, y: 2, z: 8, core: 2. Of those that a mesh axis runs over, the one named last changes fastest.
The devices are a block of a 4x4x8 slice.
Arguments:
- hidden: bfloat16 [8, 1024, 2048], P('data'), parts along dimension 0
- seg_ids: int32 [8, 1024], P('data'), parts along dimension 0
- grad_out: bfloat16 [8, 1024, 2048], P('data'), parts along dimension 0
- gain_attn: float32 [2048], replicated
- gain_mlp: float32 [2048], replicated
- w_q: bfloat16 [2048, 2048], P(None, 'tp')
- w_k: bfloat16 [2048, 128], replicated
- w_v: bfloat16 [2048, 128], replicated
- w_o: bfloat16 [2048, 2048], P('tp')
- w_gate: bfloat16 [2048, 6656], P(None, 'tp')
- w_up: bfloat16 [2048, 6656], P(None, 'tp')
- w_down: bfloat16 [6656, 2048], P('tp')
Outputs:
- output 1: bfloat16 [8, 1024, 2048], P('data'), parts along dimension 0
- output 2: bfloat16 [8, 1024, 2048], P('data'), parts along dimension 0
- output 3: float32 [8192], P('data'), parts along dimension 0
- output 4: float32 [8192], P('data'), parts along dimension 0
- output 5: float32 [8192, 2048], P('data', 'tp'), parts along dimension 0
- output 6: float32 [8192, 128], P('data'), parts along dimension 0
- output 7: float32 [8192, 128], P('data'), parts along dimension 0
- output 8: float32 [8192, 2048], P(('data', 'tp')), parts along dimension 0
- output 9: float32 [8192, 6656], P('data', 'tp'), parts along dimension 0
- output 10: float32 [8192, 6656], P('data', 'tp'), parts along dimension 0
- output 11: float32 [26624, 2048], P(('data', 'tp')), parts along dimension 0
There are 4 independent parts. A program takes and returns all parts, laid end to end along the dimension named above; an argument that names none is the same for every part.
All inputs are finite; a program needn't handle non-finite values.
Results may differ from a plain program's by a relative error of at most 0.02.
Values are sent between devices in bfloat16 or wider.
A program may use at most 768 MiB of HBM per device.

v0:
```python
import functools
import jax
import jax.numpy as jnp
from jax import lax
from jax.sharding import PartitionSpec as P

HEAD_DIM = 128
EPS = 1e-5


def rms_forward(x_in, gain):
    x_float = x_in.astype(jnp.float32)
    inv_rms = lax.rsqrt(jnp.mean(x_float * x_float, axis=-1, keepdims=True) + EPS)
    normed = x_float * inv_rms
    return (normed * gain).astype(jnp.bfloat16), normed, inv_rms


def rms_backward(grad_norm, normed, inv_rms, gain):
    grad_float = grad_norm.astype(jnp.float32)
    lead_axes = tuple(range(grad_float.ndim - 1))
    gain_grad = jnp.sum(grad_float * normed, axis=lead_axes)
    scaled = grad_float * gain
    grad_x = inv_rms * (scaled - normed * jnp.mean(scaled * normed, axis=-1, keepdims=True))
    return grad_x, gain_grad


def local_attention(q_loc, k_loc, v_loc, allowed):
    scores = jnp.einsum('bqkgd,bskd->bkgqs', q_loc, k_loc, preferred_element_type=jnp.float32) * HEAD_DIM ** -0.5
    scores = jnp.where(allowed[:, None, None], scores, -1e30)
    probs = jax.nn.softmax(scores, axis=-1).astype(jnp.bfloat16)
    return jnp.einsum('bkgqs,bskd->bqkgd', probs, v_loc, preferred_element_type=jnp.float32)


def project(acts, weight):
    return jnp.einsum('bsd,de->bse', acts, weight, preferred_element_type=jnp.float32)


def solution(mesh):
    tp_size = mesh.shape['tp']

    def device_step(hidden, seg_ids, grad_out, gain_attn, gain_mlp, w_q, w_k, w_v, w_o, w_gate, w_up, w_down):
        seq_len = hidden.shape[1]
        width = hidden.shape[2]
        loc_heads = w_q.shape[1] // HEAD_DIM
        kv_heads = w_k.shape[1] // HEAD_DIM
        group = loc_heads * tp_size // kv_heads
        kv_loc = max(1, loc_heads // group)
        grp_loc = loc_heads // kv_loc
        kv_start = lax.axis_index('tp') * loc_heads // group
        w_k_loc = lax.dynamic_slice_in_dim(w_k, kv_start * HEAD_DIM, kv_loc * HEAD_DIM, axis=1)
        w_v_loc = lax.dynamic_slice_in_dim(w_v, kv_start * HEAD_DIM, kv_loc * HEAD_DIM, axis=1)
        positions = jnp.arange(seq_len)
        allowed = (positions[:, None] >= positions[None, :])[None] & (seg_ids[:, :, None] == seg_ids[:, None, :])
        attn_fn = functools.partial(local_attention, allowed=allowed)

        def forward(x_in):
            normed_a, xn_attn, inv_attn = rms_forward(x_in, gain_attn)
            q_loc = project(normed_a, w_q).astype(jnp.bfloat16).reshape(2, seq_len, kv_loc, grp_loc, HEAD_DIM)
            k_loc = project(normed_a, w_k_loc).astype(jnp.bfloat16).reshape(2, seq_len, kv_loc, HEAD_DIM)
            v_loc = project(normed_a, w_v_loc).astype(jnp.bfloat16).reshape(2, seq_len, kv_loc, HEAD_DIM)
            ctx, attn_pull = jax.vjp(attn_fn, q_loc, k_loc, v_loc)
            ctx_b = ctx.astype(jnp.bfloat16).reshape(2, seq_len, loc_heads * HEAD_DIM)
            attn_part = jnp.einsum('bse,ed->bsd', ctx_b, w_o, preferred_element_type=jnp.float32).astype(jnp.bfloat16)
            attn_out = lax.psum(attn_part, 'tp')
            resid = (x_in.astype(jnp.float32) + attn_out.astype(jnp.float32)).astype(jnp.bfloat16)
            mixed, xn_mlp, inv_mlp = rms_forward(resid, gain_mlp)
            gate = project(mixed, w_gate)
            upper = project(mixed, w_up)
            act = (jax.nn.silu(gate) * upper).astype(jnp.bfloat16)
            mlp_part = jnp.einsum('bsf,fd->bsd', act, w_down, preferred_element_type=jnp.float32).astype(jnp.bfloat16)
            mlp_out = lax.psum(mlp_part, 'tp')
            y_out = (resid.astype(jnp.float32) + mlp_out.astype(jnp.float32)).astype(jnp.bfloat16)
            return y_out, (normed_a, xn_attn, inv_attn, ctx_b, attn_pull, xn_mlp, inv_mlp, mixed, gate, upper, act)

        def spread_kv(kv_part):
            base = jnp.zeros((width, kv_heads * HEAD_DIM), jnp.float32)
            return lax.dynamic_update_slice(base, kv_part, (0, kv_start * HEAD_DIM))

        y_out, _ = forward(hidden)
        x_again, _ = lax.optimization_barrier((hidden, y_out))
        _, kept = forward(x_again)
        normed_a, xn_attn, inv_attn, ctx_b, attn_pull, xn_mlp, inv_mlp, mixed, gate, upper, act = kept
        grad_act = jnp.einsum('bsd,fd->bsf', grad_out, w_down, preferred_element_type=jnp.float32)
        grad_w_down = jnp.einsum('bsf,bsd->fd', act, grad_out, preferred_element_type=jnp.float32)
        sigmoid_g = jax.nn.sigmoid(gate)
        grad_gate = (grad_act * upper * sigmoid_g * (1.0 + gate * (1.0 - sigmoid_g))).astype(jnp.bfloat16)
        grad_up = (grad_act * gate * sigmoid_g).astype(jnp.bfloat16)
        grad_w_gate = jnp.einsum('bsd,bsf->df', mixed, grad_gate, preferred_element_type=jnp.float32)
        grad_w_up = jnp.einsum('bsd,bsf->df', mixed, grad_up, preferred_element_type=jnp.float32)
        mixed_part = (jnp.einsum('bsf,df->bsd', grad_gate, w_gate, preferred_element_type=jnp.float32) + jnp.einsum('bsf,df->bsd', grad_up, w_up, preferred_element_type=jnp.float32)).astype(jnp.bfloat16)
        grad_mixed = lax.psum(mixed_part, 'tp')
        resid_back, grad_gain_mlp = rms_backward(grad_mixed, xn_mlp, inv_mlp, gain_mlp)
        grad_resid = grad_out.astype(jnp.float32) + resid_back
        resid_b = grad_resid.astype(jnp.bfloat16)
        grad_w_o = jnp.einsum('bse,bsd->ed', ctx_b, resid_b, preferred_element_type=jnp.float32)
        grad_ctx = jnp.einsum('bsd,ed->bse', resid_b, w_o, preferred_element_type=jnp.float32)
        grad_q, grad_k, grad_v = attn_pull(grad_ctx.reshape(2, seq_len, kv_loc, grp_loc, HEAD_DIM))
        grad_q = grad_q.reshape(2, seq_len, loc_heads * HEAD_DIM)
        grad_k = grad_k.reshape(2, seq_len, kv_loc * HEAD_DIM)
        grad_v = grad_v.reshape(2, seq_len, kv_loc * HEAD_DIM)
        grad_w_q = jnp.einsum('bsd,bse->de', normed_a, grad_q, preferred_element_type=jnp.float32)
        part_w_k = jnp.einsum('bsd,bse->de', normed_a, grad_k, preferred_element_type=jnp.float32)
        part_w_v = jnp.einsum('bsd,bse->de', normed_a, grad_v, preferred_element_type=jnp.float32)
        normed_part = (jnp.einsum('bse,de->bsd', grad_q, w_q, preferred_element_type=jnp.float32) + jnp.einsum('bse,de->bsd', grad_k, w_k_loc, preferred_element_type=jnp.float32) + jnp.einsum('bse,de->bsd', grad_v, w_v_loc, preferred_element_type=jnp.float32)).astype(jnp.bfloat16)
        grad_normed = lax.psum(normed_part, 'tp')
        input_back, grad_gain_attn = rms_backward(grad_normed, xn_attn, inv_attn, gain_attn)
        grad_in = (grad_resid + input_back).astype(jnp.bfloat16)
        grad_w_k = lax.psum(spread_kv(part_w_k), 'tp')
        grad_w_v = lax.psum(spread_kv(part_w_v), 'tp')
        return (y_out, grad_in, grad_gain_attn, grad_gain_mlp, grad_w_q, grad_w_k, grad_w_v, grad_w_o, grad_w_gate, grad_w_up, grad_w_down)

    spec_act = P('data', None, None)
    spec_rows = P('data', None)
    spec_gain = P(None)
    spec_cols = P(None, 'tp')
    spec_tprows = P('tp', None)
    spec_whole = P(None, None)
    spec_stack = P(('data', 'tp'), None)
    in_specs = (spec_act, spec_rows, spec_act, spec_gain, spec_gain, spec_cols, spec_whole, spec_whole, spec_tprows, spec_cols, spec_cols, spec_tprows)
    out_specs = (spec_act, spec_act, P('data'), P('data'), P('data', 'tp'), spec_rows, spec_rows, spec_stack, P('data', 'tp'), P('data', 'tp'), spec_stack)
    return jax.shard_map(device_step, mesh=mesh, in_specs=in_specs, out_specs=out_specs, check_vma=False)
```

profile of v0, /device:TPU:21, one launch (start us, length us, event | category | flops | bytes accessed | tf_op | source)
XLA Modules:
  0.0 1010.5 jit_solution(15174147098336244359)
XLA Ops:
  7.2 0.1 all-reduce.8.cloned.1.call-start
  7.3 0.3 iota_compare_fusion
  7.6 5.3 fusion.18
  12.9 0.2 copy-done.2
  13.2 3.5 fusion.101
  16.6 4.1 fusion.92
  20.7 10.6 %fusion.47 = (f32[2,1024]{1,0:T(2,128)S(1)}, f32[2,1024,1024]{2,1,0:T(8,128)}) fusion(s32[2,1024]{1,0:T(2,128)S(1)} %copy-done.21, pred[1024,1024]{0,1:T(8,128)(4,1)S(1)} %iota_compare_fusion, bf16[2,1024,128]{2,1,0:T(8,128)(2,1)} %fusion.101, bf16[2,1024,2048]{2,1,0:T(8,128)(2,1)} %param.12, f32[2048]{0:T(1024)S(1)} %copy-done.25, ...), kind=kOutput, calls=%fused_computation.73 | convolution fusion | flops 1638135808 | bytes 18907136 | tf_op jit(solution)/shard_map/jvp(bqkgd,bskd->bkgqs)/dot_general | solution.py:28
  31.3 5.6 fusion.40
  36.9 10.5 %convolution_convert_fusion.2 = bf16[2,1024,2048]{2,1,0:T(8,128)(2,1)} fusion(bf16[2,1024,128]{1,2,0:T(8,128)(2,1)} %fusion.92, f32[2,1024]{1,0:T(2,128)S(1)} %fusion.40, f32[2,1024]{1,0:T(2,128)S(1)} %get-tuple-element.25, f32[2,1024,1024]{2,1,0:T(8,128)} %get-tuple-element.26, s32[2,1024]{1,0:T(2,128)S(1)} %copy-done.21, ...), kind=kOutput, calls=%fused_computation.72 | convolution fusion | flops 1629749248 | bytes 18898944 | tf_op jit(solution)/shard_map/bse,ed->bsd/dot_general | solution.py:63
  47.4 0.1 all-reduce.8.cloned.1.call-update
  47.5 0.1 all-reduce.10.cloned.1.call-start
  47.6 131.6 %all-reduce.8.cloned.1.call-done = bf16[2,1024,2048]{2,1,0:T(8,128)(2,1)} async-done(((bf16[2,1024,2048]{2,1,0:T(8,128)(2,1)}), bf16[2,1024,2048]{2,1,0:T(8,128)(2,1)}) %all-reduce.8.cloned.1.call-update) | async-done | bytes 8388624 | tf_op jit(solution)/shard_map/psum | solution.py:64
  179.2 8.2 fusion.22
  187.5 3.4 copy-done.7
  190.9 5.7 fusion.45
  196.5 13.9 %convolution_convert_fusion = bf16[2,1024,2048]{2,1,0:T(8,128)(2,1)} fusion(f32[2,1024,416]{1,2,0:T(8,128)} %fusion.45, bf16[2,1024,2048]{2,1,0:T(8,128)(2,1)} %copy-done.7, f32[2048]{0:T(1024)S(1)} %copy-done.22, f32[2,1024]{1,0:T(2,128)S(1)} %add_rsqrt_fusion.2, bf16[416,2048]{1,0:T(8,128)(2,1)} %param.23, bf16[2048,416]{0,1:T(8,128)(2,1)S(1)} %copy-done), kind=kOutput, calls=%fused_computation.70 | convolution fusion | flops 7005405184 | bytes 23609344 | tf_op jit(solution)/shard_map/bsf,fd->bsd/dot_general | solution.py:70
  210.6 0.1 all-reduce.12.cloned.1.call-start
  210.6 127.9 %all-reduce.10.cloned.1.call-done = bf16[2,1024,2048]{2,1,0:T(8,128)(2,1)} async-done(((bf16[2,1024,2048]{2,1,0:T(8,128)(2,1)}), bf16[2,1024,2048]{2,1,0:T(8,128)(2,1)}) %all-reduce.10.cloned.1.call-update) | async-done | bytes 8388624 | tf_op jit(solution)/shard_map/psum | solution.py:71
  338.5 10.8 %fusion.25 = bf16[2,1024,2048]{2,1,0:T(8,128)(2,1)} fusion(bf16[2,1024,2048]{2,1,0:T(8,128)(2,1)} %copy-done.7, bf16[2,1024,2048]{2,1,0:T(8,128)(2,1)} %all-reduce.10.cloned.1.call-done), kind=kLoop, calls=%fused_computation.39 | loop fusion | flops 16777216 | bytes 25165824 | tf_op jit(solution)/shard_map/convert_element_type | solution.py:72
  349.3 5.2 fusion.29
  354.6 6.0 convolution_convert_fusion.6
  360.7 2.7 convolution_convert_fusion.7
  363.4 2.7 convolution_convert_fusion.8
  366.1 2.6 fusion.42
  368.7 3.5 fusion.148
  372.2 3.6 fusion.114
  375.9 0.8 copy-done.9
  376.7 5.6 convolution_convert_fusion.1
  382.3 0.1 all-reduce.14.cloned.1.call-start
  382.4 128.0 %all-reduce.12.cloned.1.call-done = bf16[2,1024,2048]{2,1,0:T(8,128)(2,1)} async-done(((bf16[2,1024,2048]{2,1,0:T(8,128)(2,1)}), bf16[2,1024,2048]{2,1,0:T(8,128)(2,1)}) %all-reduce.12.cloned.1.call-update) | async-done | bytes 8388624 | tf_op jit(solution)/shard_map/psum | solution.py:64
  510.4 8.2 fusion.16
  518.7 3.9 fusion.62
  522.6 0.3 copy-done.3
  522.9 5.7 fusion.64
  528.6 6.4 multiply_convert_fusion.1
  535.0 8.1 fusion.77
  543.1 10.8 %add_convert_fusion.1 = bf16[2,1024,2048]{2,1,0:T(8,128)(2,1)} fusion(f32[2,1024,2048]{2,1,0:T(8,128)} %fusion.77, bf16[2,1024,416]{1,2,0:T(8,128)(2,1)S(1)} %get-tuple-element.23, bf16[2048,416]{0,1:T(8,128)(2,1)S(1)} %copy-done), kind=kOutput, calls=%fused_computation.46 | convolution fusion | flops 3498049536 | bytes 28573696 | tf_op jit(solution)/shard_map/bsf,df->bsd/dot_general | solution.py:90
  554.0 0.1 all-reduce.16.cloned.1.call-start
  554.1 10.9 %convolution_bitcast_fusion.2 = f32[416,2048]{1,0:T(8,128)} fusion(bf16[2,1024,2048]{2,1,0:T(8,128)(2,1)} %param.14, f32[2,1024,416]{1,2,0:T(8,128)} %fusion.64, f32[2,1024,416]{1,2,0:T(8,128)} %copy-done.37), kind=kOutput, calls=%fused_computation.91 | convolution fusion | flops 3494772736 | bytes 18612224 | tf_op jit(solution)/shard_map/bsf,bsd->fd/dot_general | solution.py:84
  565.0 117.1 %all-reduce.14.cloned.1.call-done = bf16[2,1024,2048]{2,1,0:T(8,128)(2,1)} async-done(((bf16[2,1024,2048]{2,1,0:T(8,128)(2,1)}), bf16[2,1024,2048]{2,1,0:T(8,128)(2,1)}) %all-reduce.14.cloned.1.call-update) | async-done | bytes 8388624 | tf_op jit(solution)/shard_map/psum | solution.py:91
  682.1 10.8 %fusion.17 = (f32[2048]{0:T(1024)}, f32[2,1024]{1,0:T(2,128)S(1)}) fusion(bf16[2,1024,2048]{2,1,0:T(8,128)(2,1)} %copy-done.3, bf16[2,1024,2048]{2,1,0:T(8,128)(2,1)} %all-reduce.14.cloned.1.call-done, f32[2,1024]{1,0:T(2,128)S(1)} %add_rsqrt_fusion, f32[2048]{0:T(1024)S(1)} %copy-done.22), kind=kLoop, calls=%fused_computation.31 | loop fusion | flops 33550336 | bytes 16809984 | tf_op jit(solution)/shard_map/reduce_sum | solution.py:21
  692.9 9.4 fusion.41
  702.3 2.4 convolution_bitcast_fusion.7
  704.7 0.8 copy-done.5
  705.6 4.5 fusion.111
  710.1 4.5 fusion.39
  714.7 5.7 convolution_convert_fusion.4
  720.4 5.6 convolution_convert_fusion.5
  726.1 8.1 fusion.124
  734.2 8.1 fusion.120
  742.2 15.4 %add_convert_fusion = bf16[2,1024,2048]{2,1,0:T(8,128)(2,1)} fusion(f32[2,1024,2048]{2,1,0:T(8,128)} %fusion.120, f32[2,1024,2048]{2,1,0:T(8,128)} %fusion.124, bf16[2,1024,128]{1,2,0:T(8,128)(2,1)S(1)} %fusion.111, bf16[2048,128]{1,0:T(8,128)(2,1)S(1)} %copy-done.12), kind=kOutput, calls=%fused_computation.45 | convolution fusion | flops 1086324736 | bytes 42991616 | tf_op jit(solution)/shard_map/bse,de->bsd/dot_general | solution.py:104
  757.7 0.3 all-reduce.18.cloned.1.call-start
  758.0 9.6 convolution_bitcast_fusion
  767.6 9.2 convolution_bitcast_fusion.1
  776.8 2.3 convolution_bitcast_fusion.3
  779.1 4.5 convolution_bitcast_fusion.4
  783.6 4.8 convolution_bitcast_fusion.6
  788.4 4.5 convolution_bitcast_fusion.5
  793.0 92.7 %all-reduce.16.cloned.1.call-done = bf16[2,1024,2048]{2,1,0:T(8,128)(2,1)} async-done(((bf16[2,1024,2048]{2,1,0:T(8,128)(2,1)}), bf16[2,1024,2048]{2,1,0:T(8,128)(2,1)}) %all-reduce.16.cloned.1.call-update) | async-done | bytes 8388624 | tf_op jit(solution)/shard_map/psum | solution.py:105
  885.6 10.1 %fusion.28 = (f32[2048]{0:T(1024)}, f32[2,1024]{1,0:T(2,128)S(1)}) fusion(bf16[2,1024,2048]{2,1,0:T(8,128)(2,1)} %param.12, bf16[2,1024,2048]{2,1,0:T(8,128)(2,1)} %all-reduce.16.cloned.1.call-done, f32[2,1024]{1,0:T(2,128)S(1)} %copy-done.24, f32[2048]{0:T(1024)S(1)} %copy-done.26), kind=kLoop, calls=%fused_computation.42 | loop fusion | flops 33550336 | bytes 16809984 | tf_op jit(solution)/shard_map/reduce_sum | solution.py:21
  895.8 18.8 %fusion.11 = bf16[2,1024,2048]{2,1,0:T(8,128)(2,1)} fusion(bf16[2,1024,2048]{2,1,0:T(8,128)(2,1)S(1)} %copy-done.6, bf16[2,1024,2048]{2,1,0:T(8,128)(2,1)} %param.12, f32[2,1024]{1,0:T(2,128)S(1)} %broadcast_multiply_fusion, f32[2,1024]{1,0:T(2,128)S(1)} %copy-done.24, f32[2048]{0:T(1024)S(1)} %copy-done.26, f32[2,1024]{1,0:T(2,128)S(1)} %broadcast_multiply_fusion.1, ...), kind=kLoop, calls=%fused_computation.25 | loop fusion | flops 75497472 | bytes 50380800 | tf_op jit(solution)/shard_map/convert_element_type | solution.py:107
  914.6 84.1 %all-reduce.18.cloned.1.call-done = (f32[2048,128]{1,0:T(8,128)}, f32[2048,128]{1,0:T(8,128)}) async-done(((f32[2048,128]{1,0:T(8,128)}, f32[2048,128]{1,0:T(8,128)}), (f32[2048,128]{1,0:T(8,128)}, f32[2048,128]{1,0:T(8,128)})) %all-reduce.18.cloned.1.call-update) | async-done | bytes 2097168 | tf_op jit(solution)/shard_map/psum | solution.py:108
  998.6 2.3 copy.58
  1000.9 2.3 copy.59
  (113 shorter events, 0.7 us)
Async XLA Ops:
  7.2 189.4 %copy-start = (bf16[2048,416]{0,1:T(8,128)(2,1)S(1)}, bf16[2048,416]{0,1:T(8,128)(2,1)}, u32[]{:S(2)}) copy-start(bf16[2048,416]{0,1:T(8,128)(2,1)} %param.22) | copy-start | bytes 5111812
  7.2 5.7 copy-start.25
  7.2 172.0 %all-reduce.8.cloned.1.call-start = ((), (), s32[]{:S(2)}) async-start(), calls=%async_computation | async-start | bytes 16777216 | tf_op jit(solution)/shard_map/psum | solution.py:64
  7.3 5.8 copy-start.2
  7.3 5.9 copy-start.16
  13.2 3.5 copy-start.11
  16.6 4.1 copy-start.21
  47.5 143.4 %copy-start.22 = (f32[2048]{0:T(1024)S(1)}, f32[2048]{0:T(1024)}, u32[]{:S(2)}) copy-start(f32[2048]{0:T(1024)} %param.16) | copy-start | bytes 24580
  47.5 291.0 %all-reduce.10.cloned.1.call-start = ((), (), s32[]{:S(2)}) async-start(), calls=%async_computation.1 | async-start | bytes 16777216 | tf_op jit(solution)/shard_map/psum | solution.py:71
  179.2 11.7 %copy-start.28 = (bf16[2048,416]{0,1:T(8,128)(2,1)S(1)}, bf16[2048,416]{0,1:T(8,128)(2,1)}, u32[]{:S(2)}) copy-start(bf16[2048,416]{0,1:T(8,128)(2,1)} %param.21) | copy-start | bytes 5111812
  187.5 3.4 copy-start.7
  210.6 299.9 %all-reduce.12.cloned.1.call-start = ((), (), s32[]{:S(2)}) async-start(), calls=%async_computation.2 | async-start | bytes 16777216 | tf_op jit(solution)/shard_map/psum | solution.py:64
  349.3 5.3 copy-start.17
  349.3 11.3 %slice-start = ((s8[8388608]{0:T(1024)(128)(4,1)}), s8[4194304]{0:T(1024)(128)(4,1)S(1)}, s32[]{:S(2)}) async-start(s8[8388608]{0:T(1024)(128)(4,1)} %bitcast.210), calls=%async_computation.6 | async-start | bytes 8388608
  354.6 8.8 copy-start.23
  354.6 6.0 slice-start.1
  354.6 6.0 copy-start.14
  360.7 5.4 copy-start.35
  363.4 2.7 copy-start.33
  366.1 6.1 copy-start.38
  368.7 3.5 copy-start.8
  372.2 4.4 copy-start.13
  375.9 0.8 copy-start.9
  382.3 299.8 %all-reduce.14.cloned.1.call-start = ((), (), s32[]{:S(2)}) async-start(), calls=%async_computation.3 | async-start | bytes 16777216 | tf_op jit(solution)/shard_map/psum | solution.py:91
  510.4 8.2 copy-start.29
  518.6 4.2 copy-start.3
  518.7 9.9 slice-start.6
  522.9 5.7 copy-start.37
  522.9 5.7 slice-start.7
  522.9 5.7 copy-start.27
  535.0 8.2 copy-start.31
  535.0 8.1 copy-start.30
  554.0 331.6 %all-reduce.16.cloned.1.call-start = ((), (), s32[]{:S(2)}) async-start(), calls=%async_computation.4 | async-start | bytes 16777216 | tf_op jit(solution)/shard_map/psum | solution.py:105
  682.1 10.8 %copy-start.4 = (bf16[2,1024,2048]{2,1,0:T(8,128)(2,1)S(1)}, bf16[2,1024,2048]{2,1,0:T(8,128)(2,1)}, u32[]{:S(2)}) copy-start(bf16[2,1024,2048]{2,1,0:T(8,128)(2,1)} %all-reduce.14.cloned.1.call-done) | copy-start | bytes 25165828
  682.1 23.4 %slice-start.8 = ((s8[8388608]{0:T(1024)(128)(4,1)}), s8[4194304]{0:T(1024)(128)(4,1)S(1)}, s32[]{:S(2)}) async-start(s8[8388608]{0:T(1024)(128)(4,1)} %bitcast.218), calls=%async_computation.14 | async-start | bytes 8388608
  692.9 12.7 %slice-start.9 = ((s8[8388608]{0:T(1024)(128)(4,1)}), s8[4194304]{0:T(1024)(128)(4,1)S(1)}, s32[]{:S(2)}) async-start(s8[8388608]{0:T(1024)(128)(4,1)} %bitcast.218), calls=%async_computation.15 | async-start | bytes 8388608
  702.3 3.3 copy-start.5
  705.6 4.5 copy-start.39
  710.1 4.6 copy-start.36
  714.7 5.7 copy-start.34
  720.4 5.6 copy-start.15
  726.0 8.1 copy-start.19
  726.1 8.1 copy-start.18
  734.2 8.1 copy-start.12
  757.7 241.0 %all-reduce.18.cloned.1.call-start = ((), (), s32[]{:S(2)}) async-start(), calls=%async_computation.5 | async-start | bytes 4194304 | tf_op jit(solution)/shard_map/psum | solution.py:108
  757.9 9.7 copy-start.32
  758.0 18.8 %slice-start.4 = ((s8[8388608]{0:T(1024)(128)(4,1)}), s8[4194304]{0:T(1024)(128)(4,1)S(1)}, s32[]{:S(2)}) async-start(s8[8388608]{0:T(1024)(128)(4,1)} %bitcast.214), calls=%async_computation.10 | async-start | bytes 8388608
  758.0 21.1 %slice-start.2 = ((s8[8388608]{0:T(1024)(128)(4,1)}), s8[4194304]{0:T(1024)(128)(4,1)S(1)}, s32[]{:S(2)}) async-start(s8[8388608]{0:T(1024)(128)(4,1)} %bitcast.212), calls=%async_computation.8 | async-start | bytes 8388608
  767.6 9.2 slice-start.5
  767.6 9.2 copy-start.10
  767.6 11.5 %slice-start.3 = ((s8[8388608]{0:T(1024)(128)(4,1)}), s8[4194304]{0:T(1024)(128)(4,1)S(1)}, s32[]{:S(2)}) async-start(s8[8388608]{0:T(1024)(128)(4,1)} %bitcast.212), calls=%async_computation.9 | async-start | bytes 8388608
  776.8 2.3 copy-start.24
  776.8 2.3 copy-start.26
  779.1 4.5 copy-start.20
  885.6 10.1 %copy-start.6 = (bf16[2,1024,2048]{2,1,0:T(8,128)(2,1)S(1)}, bf16[2,1024,2048]{2,1,0:T(8,128)(2,1)}, u32[]{:S(2)}) copy-start(bf16[2,1024,2048]{2,1,0:T(8,128)(2,1)} %all-reduce.16.cloned.1.call-done) | copy-start | bytes 25165828
  895.8 107.4 %copy-start.1 = (bf16[2048,416]{0,1:T(8,128)(2,1)S(1)}, bf16[2048,416]{0,1:T(8,128)(2,1)}, u32[]{:S(2)}) copy-start(bf16[2048,416]{0,1:T(8,128)(2,1)} %param.22) | copy-start | bytes 5111812
Sparse Core Ops, SparseCore 0:
  47.6 131.5 all-reduce.7
  210.7 127.7 all-reduce.9
  382.4 127.9 all-reduce.11
  554.1 127.9 all-reduce.13
  757.8 127.7 all-reduce.15
  888.5 110.1 all-reduce.17
where the time goes:
time: 1010 us
  waiting for transfers between devices  682 us (68%)
  matrix products  206 us (20%)
  other arithmetic  96.4 us (10%)
  between operations  15.2 us (2%)
  local copies, waits for them, and re-layouts  10.2 us (1%)
    psum x2, waiting for transfers between devices, forward(): attn_out = lax.psum(attn_part, 'tp')  260 us
    psum x1, waiting for transfers between devices, forward(): mlp_out = lax.psum(mlp_part, 'tp')  128 us
    psum x1, waiting for transfers between devices, device_step(): grad_mixed = lax.psum(mixed_part, 'tp')  117 us
    psum x1, waiting for transfers between devices, device_step(): grad_normed = lax.psum(normed_part, 'tp')  92.7 us
    psum x1, waiting for transfers between devices, device_step(): grad_w_k = lax.psum(spread_kv(part_w_k), 'tp')  84.1 us
    dot_general x8, matrix products, project(): jnp.einsum('bsd,de->bse', acts, weight, preferred_element_type=jnp.float32)  34.1 us
    reduce_sum x4, other arithmetic, rms_forward(): jnp.mean(x_float * x_float, axis=-1, keepdims=True) + EPS  27 us
    dot_general x4, matrix products, local_attention(): jnp.einsum('bqkgd,bskd->bkgqs', q_loc, k_loc, preferred_element_type=jnp....  24.5 us
  transfers between devices with their start and end apart: 6, of which 6 were waited for; matrix products, arithmetic and copies ran while one was open for 7% of the time, Pallas kernels for 0%

commit v1 on v0

v1 whole, which is shorter than its diff:
```python
import functools
import jax
import jax.numpy as jnp
from jax import lax
from jax.experimental import pallas as pl
from jax.experimental.pallas import tpu as pltpu
from jax.sharding import PartitionSpec as P

HEAD_DIM = 128
EPS = 1e-5
SUB = 4
ROWS = 16
BLK = 256
BF = jnp.bfloat16
F32 = jnp.float32
MESH = pl.DeviceIdType.MESH
VMEM_LIMIT = 60 * 1024 * 1024


def mm(a, b):
    return lax.dot_general(a, b, (((1,), (0,)), ((), ())), preferred_element_type=F32)


def mm_nt(a, b):
    return lax.dot_general(a, b, (((1,), (1,)), ((), ())), preferred_element_type=F32)


def mm_tn(a, b):
    return lax.dot_general(a, b, (((0,), (0,)), ((), ())), preferred_element_type=F32)


def rms_parts(x_in):
    x_float = x_in.astype(F32)
    inv = lax.rsqrt(jnp.mean(x_float * x_float, axis=-1, keepdims=True) + EPS)
    return x_float * inv, inv


def rms_back(grad, normed, inv, gain):
    scaled = grad * gain
    return inv * (scaled - normed * jnp.mean(scaled * normed, axis=-1, keepdims=True))


def ring_kernel(chips, n_in, n_out, epilogue, with_gain, part, *refs):
    ins = refs[:n_in]
    out = refs[n_in]
    outs = refs[n_in + 1:n_in + 1 + n_out]
    scratch = refs[n_in + 1 + n_out:]
    (loc, oth, arr, gat, ld_sem, xs_sem, xr_sem, rs_sem, rr_sem, as_sem, ar_sem, ps_sem, pr_sem, wo_sem) = scratch[:14]
    me = lax.axis_index('tp')
    chip = me // 2
    core = me % 2
    mate = chip * 2 + 1 - core
    nxt = (lax.rem(chip + 1, chips) * 2 + core, lax.rem(chip + chips - 1, chips) * 2 + core)

    def dev(t):
        return {'tp': t}

    barrier = pltpu.get_barrier_semaphore()
    for t in (nxt[0], nxt[1], mate):
        pl.semaphore_signal(barrier, inc=1, device_id=dev(t), device_id_type=MESH)
    pl.semaphore_wait(barrier, 3)

    def chunk_at(d, s):
        off = s if d == 1 else chips - s
        return lax.rem(chip + off, chips)

    def swap(d, s):
        m = chunk_at(d, s)
        return pltpu.make_async_remote_copy(
            src_ref=part.at[m * 2 + 1 - core, d], dst_ref=oth.at[m, d], send_sem=xs_sem,
            recv_sem=xr_sem.at[m, d], device_id=dev(mate), device_id_type=MESH)

    def load(d, s):
        m = chunk_at(d, s)
        return pltpu.make_async_copy(part.at[m * 2 + core, d], loc.at[m, d], ld_sem.at[m, d])

    if with_gain:
        (gacc, gbuf, gmate, gs_sem, gr_sem, gms_sem, gmr_sem, kacc, koth, karr, kxs, kxr, krs, krr, kas, kar, kps, kpr) = scratch[14:]
        kin, kout = ins[5], outs[1]

        def kswap(d, s):
            m = chunk_at(d, s)
            return pltpu.make_async_remote_copy(
                src_ref=kin.at[m * 2 + 1 - core, d], dst_ref=koth.at[m, d], send_sem=kxs,
                recv_sem=kxr.at[m, d], device_id=dev(mate), device_id_type=MESH)

        def krs_copy(d, s, m):
            return pltpu.make_async_remote_copy(
                src_ref=kacc.at[m, d], dst_ref=karr.at[s, d], send_sem=krs,
                recv_sem=krr.at[s, d], device_id=dev(nxt[d]), device_id_type=MESH)

        def kag_copy(d, t, m):
            return pltpu.make_async_remote_copy(
                src_ref=kout.at[m * 2 + core, d], dst_ref=kout.at[m * 2 + core, d], send_sem=kas,
                recv_sem=kar.at[t, d], device_id=dev(nxt[d]), device_id_type=MESH)

        def kspread(d, m):
            pltpu.make_async_remote_copy(
                src_ref=kout.at[m * 2 + core, d], dst_ref=kout.at[m * 2 + core, d], send_sem=kps,
                recv_sem=kpr, device_id=dev(mate), device_id_type=MESH).start()

    for s in range(1, chips + 1):
        for d in range(2):
            swap(d, s % chips).start()
            load(d, s % chips).start()
            if with_gain:
                kswap(d, s % chips).start()

    def rs_copy(d, j, s, m):
        return pltpu.make_async_remote_copy(
            src_ref=loc.at[m, d, j], dst_ref=arr.at[s, d, j], send_sem=rs_sem,
            recv_sem=rr_sem.at[s, d, j], device_id=dev(nxt[d]), device_id_type=MESH)

    def ready(d, s):
        load(d, s).wait()
        swap(d, s).wait_recv()

    def rs_step(s, first):
        for d in range(2):
            ready(d, s + 1)
        for j in range(SUB):
            for d in range(2):
                m = chunk_at(d, s + 1)
                v = loc[m, d, j].astype(F32) + oth[m, d, j].astype(F32)
                if not first:
                    rs_copy(d, j, s - 1, m).wait_recv()
                    v = v + arr[s - 1, d, j].astype(F32)
                loc[m, d, j] = v.astype(BF)
                rs_copy(d, j, s, m).start()
        if with_gain:
            for d in range(2):
                m = chunk_at(d, s + 1)
                kswap(d, s + 1).wait_recv()
                kv = kin[m * 2 + core, d] + koth[m, d]
                if not first:
                    krs_copy(d, s - 1, m).wait_recv()
                    kv = kv + karr[s - 1, d]
                kacc[m, d] = kv
                krs_copy(d, s, m).start()

    rs_step(0, True)

    @pl.loop(1, chips - 1)
    def _(s):
        rs_step(s, False)

    def ag_copy(d, j, t, m):
        return pltpu.make_async_remote_copy(
            src_ref=gat.at[m, d, j], dst_ref=gat.at[m, d, j], send_sem=as_sem,
            recv_sem=ar_sem.at[t, d, j], device_id=dev(nxt[d]), device_id_type=MESH)

    def spread(d, j, m):
        pltpu.make_async_remote_copy(
            src_ref=gat.at[m, d, j], dst_ref=out.at[m * 2 + core, d, j], send_sem=ps_sem,
            recv_sem=pr_sem, device_id=dev(mate), device_id_type=MESH).start()
        pltpu.make_async_copy(gat.at[m, d, j], out.at[m * 2 + core, d, j], wo_sem).start()

    for d in range(2):
        ready(d, 0)
    state = epilogue.begin(ins, outs)
    for j in range(SUB):
        for d in range(2):
            rs_copy(d, j, chips - 2, chip).wait_recv()
            v = loc[chip, d, j].astype(F32) + oth[chip, d, j].astype(F32) + arr[chips - 2, d, j].astype(F32)
            res, state = epilogue.piece(v.astype(BF).astype(F32), d, j, ins, outs, state)
            gat[chip, d, j] = res
            ag_copy(d, j, 0, chip).start()
            spread(d, j, chip)
    epilogue.end(outs, state)

    if with_gain:
        for d in range(2):
            kswap(d, 0).wait_recv()
            krs_copy(d, chips - 2, chip).wait_recv()
            kout[chip * 2 + core, d] = kin[chip * 2 + core, d] + koth[chip, d] + karr[chips - 2, d]
            kag_copy(d, 0, chip).start()
            kspread(d, chip)

        def gain_copy(t, src):
            return pltpu.make_async_remote_copy(
                src_ref=src, dst_ref=gbuf.at[t], send_sem=gs_sem.at[t],
                recv_sem=gr_sem.at[t], device_id=dev(nxt[0]), device_id_type=MESH)

        gacc[0:1] = ins[4][...]
        gacc[1:2] = state
        gain_copy(0, gacc).start()

    def ag_step(t, last):
        for j in range(SUB):
            for d in range(2):
                m = chunk_at(d, t)
                ag_copy(d, j, t - 1, m).wait_recv()
                if not last:
                    ag_copy(d, j, t, m).start()
                spread(d, j, m)
        if with_gain:
            for d in range(2):
                m = chunk_at(d, t)
                kag_copy(d, t - 1, m).wait_recv()
                if not last:
                    kag_copy(d, t, m).start()
                kspread(d, m)
            gain_copy(t - 1, gacc).wait_recv()
            if not last:
                gain_copy(t, gbuf.at[t - 1]).start()

    @pl.loop(1, chips - 1)
    def _(t):
        ag_step(t, False)

    ag_step(chips - 1, True)

    if with_gain:
        tot = gacc[...]
        for t in range(chips - 1):
            tot = tot + gbuf[t]
            gain_copy(t, gacc).wait_send()
        outs[0][...] = tot
        mate_copy = pltpu.make_async_remote_copy(
            src_ref=outs[0], dst_ref=gmate, send_sem=gms_sem, recv_sem=gmr_sem,
            device_id=dev(mate), device_id_type=MESH)
        mate_copy.start()
        mate_copy.wait()
        outs[0][...] = tot + gmate[...]

    def bulk(ref, sem, rsem):
        return pltpu.make_async_remote_copy(
            src_ref=ref, dst_ref=ref, send_sem=sem, recv_sem=rsem, device_id=dev(mate), device_id_type=MESH)

    if with_gain:
        bulk(koth, kps, kpr).wait_recv()
        bulk(koth, kxs, kpr).wait_send()
        bulk(karr, krs, kpr).wait_send()
        bulk(karr, kas, kpr).wait_send()
        bulk(koth, kps, kpr).wait_send()
    bulk(gat, ps_sem, pr_sem).wait_recv()
    bulk(oth, xs_sem, pr_sem).wait_send()
    bulk(arr, rs_sem, pr_sem).wait_send()
    bulk(arr, as_sem, pr_sem).wait_send()
    bulk(gat, ps_sem, pr_sem).wait_send()
    pltpu.make_async_copy(gat, gat, wo_sem).wait()


class ForwardTail:
    @staticmethod
    def begin(ins, outs):
        return None

    @staticmethod
    def piece(v, d, j, ins, outs, state):
        h = (ins[0][d, j].astype(F32) + v).astype(BF)
        outs[0][d, j] = h
        normed, _ = rms_parts(h)
        return (normed * ins[1][...]).astype(BF), state

    @staticmethod
    def end(outs, state):
        pass


class AddTail:
    @staticmethod
    def begin(ins, outs):
        return None

    @staticmethod
    def piece(v, d, j, ins, outs, state):
        return (ins[0][d, j].astype(F32) + v).astype(BF), state

    @staticmethod
    def end(outs, state):
        pass


class MlpTail:
    @staticmethod
    def begin(ins, outs):
        return jnp.zeros(ins[2].shape, F32)

    @staticmethod
    def piece(v, d, j, ins, outs, state):
        normed, inv = rms_parts(ins[0][d, j])
        state = state + jnp.sum(v * normed, axis=0, keepdims=True)
        grad = ins[1][d, j].astype(F32) + rms_back(v, normed, inv, ins[2][...])
        outs[0][d, j] = grad
        return grad.astype(BF), state

    @staticmethod
    def end(outs, state):
        outs[1][...] = state


class AttnTail:
    @staticmethod
    def begin(ins, outs):
        return jnp.zeros(ins[2].shape, F32)

    @staticmethod
    def piece(v, d, j, ins, outs, state):
        normed, inv = rms_parts(ins[0][d, j])
        state = state + jnp.sum(v * normed, axis=0, keepdims=True)
        grad = ins[1][d, j] + rms_back(v, normed, inv, ins[2][...])
        return grad.astype(BF), state

    @staticmethod
    def end(outs, state):
        pass


def ring_call(part, ins, out_shapes, epilogue, chips, cid, with_gain=False):
    tokens, width = part.shape
    shape = (chips * 2, 2, SUB, ROWS, width)
    half = (chips, 2, SUB, ROWS, width)
    arrive = (chips - 1, 2, SUB, ROWS, width)
    vm = pl.BlockSpec(memory_space=pltpu.VMEM)
    anyspec = pl.BlockSpec(memory_space=pl.ANY)
    dma = pltpu.SemaphoreType.DMA
    scratch = [
        pltpu.VMEM(half, BF), pltpu.VMEM(half, BF), pltpu.VMEM(arrive, BF), pltpu.VMEM(half, BF),
        dma((chips, 2)), dma, dma((chips, 2)), dma, dma((chips - 1, 2, SUB)), dma,
        dma((chips - 1, 2, SUB)), dma, dma, dma]
    if with_gain:
        scratch += [pltpu.VMEM((2, width), F32), pltpu.VMEM((chips - 1, 2, width), F32), pltpu.VMEM((2, width), F32),
                    dma((chips - 1,)), dma((chips - 1,)), dma, dma]
        kshape = ins[5].shape[1:]
        scratch += [pltpu.VMEM((chips,) + kshape, F32), pltpu.VMEM((chips,) + kshape, F32), pltpu.VMEM((chips - 1,) + kshape, F32),
                    dma, dma((chips, 2)), dma, dma((chips - 1, 2)), dma, dma((chips - 1, 2)), dma, dma]
    n_in, n_out = len(ins), len(out_shapes)

    def body(*refs):
        ring_kernel(chips, n_in, n_out, epilogue, with_gain, *refs)

    res = pl.pallas_call(
        body,
        out_shape=[jax.ShapeDtypeStruct(shape, BF)] + out_shapes,
        in_specs=[anyspec] + [vm] * n_in,
        out_specs=[anyspec] + [vm] * n_out,
        scratch_shapes=scratch,
        name='ring_%d' % cid,
        compiler_params=pltpu.CompilerParams(collective_id=cid, has_side_effects=True, vmem_limit_bytes=VMEM_LIMIT),
        cost_estimate=pl.CostEstimate(flops=80_000_000_000, bytes_accessed=4 * tokens * width, transcendentals=0),
    )(part.reshape(shape), *ins)
    return (res[0].reshape(tokens, width),) + tuple(res[1:])


def masked_probs(q, k, seg_ref, b, row0):
    n = q.shape[0]
    seg_k = seg_ref[pl.ds(b, 1), :].astype(F32)
    own = seg_ref[pl.ds(b, 1), pl.ds(row0, n)].astype(F32)
    seg_q = jnp.transpose(jnp.broadcast_to(own, (128, n)))[:, :1]
    s = mm_nt(q, k) * HEAD_DIM ** -0.5
    rows = row0 + lax.broadcasted_iota(jnp.int32, s.shape, 0)
    cols = lax.broadcasted_iota(jnp.int32, s.shape, 1)
    s = jnp.where((rows >= cols) & (seg_q == seg_k), s, -1e30)
    e = jnp.exp(s - jnp.max(s, axis=-1, keepdims=True))
    return e * (1.0 / jnp.sum(e, axis=-1, keepdims=True))


def pack(w_ref, wq_ref, wk_ref, wv_ref):
    for n, ref in enumerate((wq_ref, wk_ref, wv_ref)):
        w_ref[:, n * HEAD_DIM:(n + 1) * HEAD_DIM] = ref[...]


def front_kernel(x_ref, sg_ref, g_ref, wq_ref, wk_ref, wv_ref, wo_ref, o_ref, qkv_ref, ctx_ref, k_s, v_s, w_ref):
    qi = pl.program_id(1)

    @pl.when((qi == 0) & (pl.program_id(0) == 0))
    def _():
        k_s[...] = jnp.zeros_like(k_s)
        v_s[...] = jnp.zeros_like(v_s)
        pack(w_ref, wq_ref, wk_ref, wv_ref)

    normed, _ = rms_parts(x_ref[0])
    a = (normed * g_ref[...]).astype(BF)
    qkv = mm(a, w_ref[...]).astype(BF)
    qkv_ref[0] = qkv
    row0 = pl.multiple_of(qi * BLK, BLK)
    k_s[pl.ds(row0, BLK)] = qkv[:, HEAD_DIM:2 * HEAD_DIM]
    v_s[pl.ds(row0, BLK)] = qkv[:, 2 * HEAD_DIM:]
    probs = masked_probs(qkv[:, :HEAD_DIM], k_s[...], sg_ref, pl.program_id(0), row0)
    ctx = mm(probs.astype(BF), v_s[...]).astype(BF)
    ctx_ref[0] = ctx
    o_ref[0] = mm(ctx, wo_ref[...]).astype(BF)


def front_call(x, seg, gain, w_q, w_k, w_v, w_o):
    nb, seq, width = x.shape
    e3 = 3 * HEAD_DIM
    rowblk = lambda n: pl.BlockSpec((1, BLK, n), lambda b, i: (b, i, 0))
    whole = lambda arr: pl.BlockSpec(arr.shape, lambda b, i: (0, 0))
    return pl.pallas_call(
        front_kernel,
        grid=(nb, seq // BLK),
        in_specs=[rowblk(width), whole(seg), whole(gain), whole(w_q), whole(w_k), whole(w_v), whole(w_o)],
        out_specs=[rowblk(width), rowblk(e3), rowblk(HEAD_DIM)],
        out_shape=[jax.ShapeDtypeStruct((nb, seq, width), BF), jax.ShapeDtypeStruct((nb, seq, e3), BF),
                   jax.ShapeDtypeStruct((nb, seq, HEAD_DIM), BF)],
        scratch_shapes=[pltpu.VMEM((seq, HEAD_DIM), BF), pltpu.VMEM((seq, HEAD_DIM), BF), pltpu.VMEM((width, e3), BF)],
        name='front',
        compiler_params=pltpu.CompilerParams(vmem_limit_bytes=VMEM_LIMIT),
        cost_estimate=pl.CostEstimate(flops=8_000_000_000, bytes_accessed=20_000_000, transcendentals=0),
    )(x, seg, gain, w_q, w_k, w_v, w_o)


def back_kernel(dr_ref, x_ref, sg_ref, g_ref, wq_ref, wk_ref, wv_ref, wo_ref, q_ref, qkv_ref, ctx_ref,
                ga_ref, dwq_ref, dkv_ref, dwo_ref, dqkv_s, dk_s, dv_s, w_ref):
    b, ph = pl.program_id(0), pl.program_id(1)
    nq = pl.num_programs(1) // 2
    scale = HEAD_DIM ** -0.5

    @pl.when((ph == 0) & (b == 0))
    def _():
        pack(w_ref, wq_ref, wk_ref, wv_ref)
        dwq_ref[...] = jnp.zeros_like(dwq_ref)
        dkv_ref[...] = jnp.zeros_like(dkv_ref)
        dwo_ref[...] = jnp.zeros_like(dwo_ref)

    @pl.when(ph == 0)
    def _():
        dk_s[...] = jnp.zeros_like(dk_s)
        dv_s[...] = jnp.zeros_like(dv_s)

    @pl.when(ph < nq)
    def _():
        row0 = pl.multiple_of(ph * BLK, BLK)
        dr = dr_ref[0]
        dctx = mm_nt(dr, wo_ref[...]).astype(BF)
        dwo_ref[...] += mm_tn(ctx_ref[0], dr)
        q = q_ref[0]
        k = qkv_ref[0, :, HEAD_DIM:2 * HEAD_DIM]
        v = qkv_ref[0, :, 2 * HEAD_DIM:]
        probs = masked_probs(q, k, sg_ref, b, row0)
        dp = mm_nt(dctx, v)
        ds = (probs * (dp - jnp.sum(dp * probs, axis=-1, keepdims=True)) * scale).astype(BF)
        dv_s[...] += mm_tn(probs.astype(BF), dctx)
        dk_s[...] += mm_tn(ds, q)
        dqkv_s[pl.ds(row0, BLK), :HEAD_DIM] = mm(ds, k).astype(BF)

    @pl.when(ph == nq - 1)
    def _():
        dqkv_s[:, HEAD_DIM:2 * HEAD_DIM] = dk_s[...].astype(BF)
        dqkv_s[:, 2 * HEAD_DIM:] = dv_s[...].astype(BF)

    @pl.when(ph >= nq)
    def _():
        row0 = pl.multiple_of((ph - nq) * BLK, BLK)
        normed, _ = rms_parts(x_ref[0])
        a = (normed * g_ref[...]).astype(BF)
        blk = dqkv_s[pl.ds(row0, BLK)]
        dw = mm_tn(a, blk)
        dwq_ref[...] += dw[:, :HEAD_DIM]
        dkv_ref[...] += dw[:, HEAD_DIM:]
        ga_ref[0] = mm_nt(blk, w_ref[...]).astype(BF)


def back_call(dr, x, seg, gain, w_q, w_k, w_v, w_o, qkv, ctx):
    nb, seq, width = x.shape
    nq = seq // BLK
    e3 = 3 * HEAD_DIM
    first = lambda n: pl.BlockSpec((1, BLK, n), lambda b, i: (b, jnp.minimum(i, nq - 1), 0))
    second = lambda n: pl.BlockSpec((1, BLK, n), lambda b, i: (b, jnp.maximum(i - nq, 0), 0))
    whole = lambda arr: pl.BlockSpec(arr.shape, lambda b, i: (0, 0))
    const = lambda shp: pl.BlockSpec(shp, lambda b, i: (0, 0))
    return pl.pallas_call(
        back_kernel,
        grid=(nb, 2 * nq),
        in_specs=[first(width), second(width), whole(seg), whole(gain), whole(w_q), whole(w_k), whole(w_v), whole(w_o),
                  first(HEAD_DIM), pl.BlockSpec((1, seq, e3), lambda b, i: (b, 0, 0)), first(HEAD_DIM)],
        out_specs=[second(width), const((width, HEAD_DIM)), const((width, 2 * HEAD_DIM)), const((HEAD_DIM, width))],
        out_shape=[jax.ShapeDtypeStruct((nb, seq, width), BF), jax.ShapeDtypeStruct((width, HEAD_DIM), F32),
                   jax.ShapeDtypeStruct((width, 2 * HEAD_DIM), F32),
                   jax.ShapeDtypeStruct((HEAD_DIM, width), F32)],
        scratch_shapes=[pltpu.VMEM((seq, e3), BF), pltpu.VMEM((seq, HEAD_DIM), F32), pltpu.VMEM((seq, HEAD_DIM), F32), pltpu.VMEM((width, e3), BF)],
        name='back',
        compiler_params=pltpu.CompilerParams(vmem_limit_bytes=VMEM_LIMIT),
        cost_estimate=pl.CostEstimate(flops=12_000_000_000, bytes_accessed=30_000_000, transcendentals=0),
    )(dr, x, seg, gain, w_q, w_k, w_v, w_o, qkv, qkv, ctx)


def mlp_kernel(m_ref, dy_ref, wg_ref, wu_ref, wd_ref, p_ref, gm_ref, dwg_ref, dwu_ref, dwd_ref):
    @pl.when(pl.program_id(0) == 0)
    def _():
        dwg_ref[...] = jnp.zeros_like(dwg_ref)
        dwu_ref[...] = jnp.zeros_like(dwu_ref)
        dwd_ref[...] = jnp.zeros_like(dwd_ref)

    m = m_ref[...]
    dy = dy_ref[...]
    gate = mm_nt(m, wg_ref[...])
    upper = mm_nt(m, wu_ref[...])
    sig = jax.nn.sigmoid(gate)
    act = (gate * sig * upper).astype(BF)
    p_ref[...] = mm(act, wd_ref[...]).astype(BF)
    dact = mm_nt(dy, wd_ref[...])
    dwd_ref[...] += mm_tn(act, dy)
    dgate = (dact * upper * sig * (1.0 + gate * (1.0 - sig))).astype(BF)
    dupper = (dact * gate * sig).astype(BF)
    dwg_ref[...] += mm_tn(dgate, m)
    dwu_ref[...] += mm_tn(dupper, m)
    gm_ref[...] = (mm(dgate, wg_ref[...]) + mm(dupper, wu_ref[...])).astype(BF)


def mlp_call(m, dy, w_gate, w_up, w_down):
    tokens, width = m.shape
    ff = w_down.shape[0]
    rowblk = pl.BlockSpec((BLK, width), lambda i: (i, 0))
    const = lambda shp: pl.BlockSpec(shp, lambda i: (0, 0))
    return pl.pallas_call(
        mlp_kernel,
        grid=(tokens // BLK,),
        in_specs=[rowblk, rowblk, const((ff, width)), const((ff, width)), const((ff, width))],
        out_specs=[rowblk, rowblk, const((ff, width)), const((ff, width)), const((ff, width))],
        out_shape=[jax.ShapeDtypeStruct((tokens, width), BF), jax.ShapeDtypeStruct((tokens, width), BF),
                   jax.ShapeDtypeStruct((ff, width), F32), jax.ShapeDtypeStruct((ff, width), F32),
                   jax.ShapeDtypeStruct((ff, width), F32)],
        name='mlp',
        compiler_params=pltpu.CompilerParams(vmem_limit_bytes=VMEM_LIMIT),
        cost_estimate=pl.CostEstimate(flops=32_000_000_000, bytes_accessed=50_000_000, transcendentals=0),
    )(m, dy, w_gate, w_up, w_down)


def solution(mesh):
    tp_size = mesh.shape['tp']
    chips = tp_size // 2

    def device_step(hidden, seg_ids, grad_out, gain_attn, gain_mlp, w_q, w_k, w_v, w_o, w_gate, w_up, w_down):
        nb, seq, width = hidden.shape
        tokens = nb * seq
        own = tokens // tp_size
        row0 = lax.axis_index('tp') * own
        piece = (2, SUB, ROWS, width)

        def own_rows(arr):
            return lax.dynamic_slice_in_dim(arr.reshape(tokens, width), row0, own, axis=0).reshape(piece)

        g1 = gain_attn[None, :]
        g2 = gain_mlp[None, :]
        x_own = own_rows(hidden)
        dy_own = own_rows(grad_out)
        shard_bf = jax.ShapeDtypeStruct(piece, BF)
        shard_f = jax.ShapeDtypeStruct(piece, F32)
        gain_f = jax.ShapeDtypeStruct((1, width), F32)
        weights = (w_q, w_k, w_v, w_o)

        o_part, qkv, ctx = front_call(hidden, seg_ids, g1, *weights)
        mixed, h_own = ring_call(o_part.reshape(tokens, width), [x_own, g2], [shard_bf], ForwardTail, chips, 1)
        p_part, gm_part, d_gate, d_up, d_down = mlp_call(mixed, grad_out.reshape(tokens, width), w_gate.T, w_up.T, w_down)
        dres, dres_own, g2_part = ring_call(gm_part, [h_own, dy_own, g2], [shard_f, gain_f], MlpTail, chips, 2)
        ga_part, d_q, d_kv, d_o = back_call(dres.reshape(nb, seq, width), hidden, seg_ids, g1, *weights, qkv, ctx)
        (y_out,) = ring_call(p_part, [h_own], [], AddTail, chips, 4)
        kv_rows = own // 2
        kv_shape = (tp_size, 2, kv_rows, 2 * HEAD_DIM)
        dx, gains, d_kv = ring_call(ga_part.reshape(tokens, width), [x_own, dres_own, g1, g1, g2_part, d_kv.reshape(kv_shape)],
                                    [jax.ShapeDtypeStruct((2, width), F32), jax.ShapeDtypeStruct(kv_shape, F32)], AttnTail, chips, 3, True)
        d_kv = d_kv.reshape(width, 2 * HEAD_DIM)
        return (y_out.reshape(nb, seq, width), dx.reshape(nb, seq, width), gains[1], gains[0], d_q, d_kv[:, :HEAD_DIM], d_kv[:, HEAD_DIM:],
                d_o, d_gate.T, d_up.T, d_down)

    spec_act = P('data', None, None)
    spec_rows = P('data', None)
    spec_gain = P(None)
    spec_cols = P(None, 'tp')
    spec_tprows = P('tp', None)
    spec_whole = P(None, None)
    spec_stack = P(('data', 'tp'), None)
    in_specs = (spec_act, spec_rows, spec_act, spec_gain, spec_gain, spec_cols, spec_whole, spec_whole, spec_tprows, spec_cols, spec_cols, spec_tprows)
    out_specs = (spec_act, spec_act, P('data'), P('data'), P('data', 'tp'), spec_rows, spec_rows, spec_stack, P('data', 'tp'), P('data', 'tp'), spec_stack)
    return jax.shard_map(device_step, mesh=mesh, in_specs=in_specs, out_specs=out_specs, check_vma=False)
```

time: 1010 us -> 512 us (0.51)
  waiting for transfers between devices: 682 us -> 0 us
  Pallas kernels: 0 us -> 488 us
  matrix products: 206 us -> 0 us
  other arithmetic: 96.4 us -> 0 us
  between operations: 15.2 us -> 0.68 us
  local copies, waits for them, and re-layouts: 10.2 us -> 23.6 us
    psum x6 -> x0, waiting for transfers between devices: 681 us -> none  [the longest x2 260 us: forward(): attn_out = lax.psum(attn_part, 'tp')]
    pallas_call x0 -> x7, Pallas kernels: none -> 488 us  [the longest x4 385 us: ring_call(): pl.pallas_call(body, out_shape=[jax.ShapeDtypeStruct(shape, BF)] + out_sh...]
    dot_general x32 -> x0, matrix products: 206 us -> none  [the longest x8 34.1 us: project(): jnp.einsum('bsd,de->bse', acts, weight, preferred_element_type=jnp.float32)]
    reduce_sum x8 -> x0, other arithmetic: 56.9 us -> none  [the longest x4 27 us: rms_forward(): jnp.mean(x_float * x_float, axis=-1, keepdims=True) + EPS]
    convert_element_type x3 -> x0, other arithmetic: 39.1 us -> none  [the longest x1 18.8 us: device_step(): grad_in = (grad_resid + input_back).astype(jnp.bfloat16)]
  transfers between devices with their start and end apart: 6 -> 0, of which waited for: 6 -> 0; matrix products, arithmetic and copies ran while one was open for 7% -> 0% of each run, Pallas kernels for 0% -> 0%
where the time goes in v1:
time: 512 us
  Pallas kernels  488 us (95%)
  local copies, waits for them, and re-layouts  23.6 us (5%)
    pallas_call x4, Pallas kernels, ring_call(): pl.pallas_call(body, out_shape=[jax.ShapeDtypeStruct(shape, BF)] + out_sh...  385 us
    pallas_call x1, Pallas kernels, mlp_call(): pl.pallas_call(mlp_kernel, grid=(tokens // BLK,), in_specs=[rowblk, rowbl...  46.6 us
    pallas_call x1, Pallas kernels, back_call(): pl.pallas_call(back_kernel, grid=(nb, 2 * nq), in_specs=[first(width), se...  35.2 us
    pallas_call x1, Pallas kernels, front_call(): pl.pallas_call(front_kernel, grid=(nb, seq // BLK), in_specs=[rowblk(widt...  20.8 us
    unnamed x2, local copies, waits for them, and re-layouts  16.9 us

profile of v1, /device:TPU:21, one launch (start us, length us, event | category | flops | bytes accessed | tf_op | source)
XLA Modules:
  0.0 512.0 jit_solution(10414193732358080039)
XLA Ops:
  0.6 2.3 constant_dynamic-slice_fusion
  2.9 20.8 %front.1 = (bf16[2,1024,2048]{2,1,0:T(8,128)(2,1)}, bf16[2,1024,384]{2,1,0:T(8,128)(2,1)}, bf16[2,1024,128]{2,1,0:T(8,128)(2,1)}) custom-call(bf16[2,1024,2048]{2,1,0:T(8,128)(2,1)} %x_ref.3, s32[2,1024]{1,0:T(2,128)} %sg_ref.3, f32[1,2048]{1,0:T(1,128)} %bitcast.37, bf16[2048,128]{1,0:T(8,128)(2,1)} %wq_ref.3, bf16[2048,128]{1,0:T(8,128)(2,1)} %wk_ref.3, ...), custom_call_target="tpu_custom_call" | custom-call | flops 8000000000 | bytes 20000000 | tf_op jit(solution)/shard_map/front/pallas_call | solution.py:391
  23.7 94.7 %ring_1.1 = (bf16[16,2,4,16,2048]{4,3,2,1,0:T(8,128)(2,1)}, bf16[2,4,16,2048]{3,2,1,0:T(8,128)(2,1)}) custom-call(bf16[16,2,4,16,2048]{4,3,2,1,0:T(8,128)(2,1)} %bitcast.46, bf16[2,4,16,2048]{3,2,1,0:T(8,128)(2,1)} %bitcast.25, f32[1,2048]{1,0:T(1,128)} %bitcast.35), custom_call_target="tpu_custom_call" | custom-call | flops 80000000000 | bytes 16777216 | tf_op jit(solution)/shard_map/ring_1/pallas_call | solution.py:333
  118.4 46.6 %mlp.1 = (bf16[2048,2048]{1,0:T(8,128)(2,1)}, bf16[2048,2048]{1,0:T(8,128)(2,1)}, f32[416,2048]{1,0:T(8,128)}, f32[416,2048]{1,0:T(8,128)}, f32[416,2048]{1,0:T(8,128)}) custom-call(bf16[2048,2048]{1,0:T(8,128)(2,1)} %bitcast.44, bf16[2048,2048]{1,0:T(8,128)(2,1)} %bitcast.29, bf16[416,2048]{1,0:T(8,128)(2,1)} %bitcast.33, bf16[416,2048]{1,0:T(8,128)(2,1)} %bitcast.34, ...), custom_call_target="tpu_custom_call" | custom-call | flops 32000000000 | bytes 50000000 | tf_op jit(solution)/shard_map/mlp/pallas_call | solution.py:508
  165.0 88.0 %ring_4.1 = bf16[16,2,4,16,2048]{4,3,2,1,0:T(8,128)(2,1)} custom-call(bf16[16,2,4,16,2048]{4,3,2,1,0:T(8,128)(2,1)} %bitcast.45, bf16[2,4,16,2048]{3,2,1,0:T(8,128)(2,1)} %get-tuple-element.34.refs_1_), custom_call_target="tpu_custom_call" | custom-call | flops 80000000000 | bytes 16777216 | tf_op jit(solution)/shard_map/ring_4/pallas_call | solution.py:333
  253.1 89.2 %ring_2.1 = (bf16[16,2,4,16,2048]{4,3,2,1,0:T(8,128)(2,1)}, f32[2,4,16,2048]{3,2,1,0:T(8,128)}, f32[1,2048]{1,0:T(1,128)}) custom-call(bf16[16,2,4,16,2048]{4,3,2,1,0:T(8,128)(2,1)} %bitcast.42, bf16[2,4,16,2048]{3,2,1,0:T(8,128)(2,1)} %get-tuple-element.34.refs_1_, bf16[2,4,16,2048]{3,2,1,0:T(8,128)(2,1)} %bitcast.27, f32[1,2048]{1,0:T(1,128)} %bitcast.36), custom_call_target="tpu_custom_call" | custom-call | flops 80000000000 | bytes 16777216 | tf_op jit(solution)/shard_map/ring_2/pallas_call | solution.py:333
  342.3 35.2 %back.1 = (bf16[2,1024,2048]{2,1,0:T(8,128)(2,1)}, f32[2048,128]{1,0:T(8,128)}, f32[2048,256]{1,0:T(8,128)}, f32[128,2048]{1,0:T(8,128)}) custom-call(bf16[2,1024,2048]{2,1,0:T(8,128)(2,1)} %bitcast.43, bf16[2,1024,2048]{2,1,0:T(8,128)(2,1)} %x_ref.3, s32[2,1024]{1,0:T(2,128)} %sg_ref.3, f32[1,2048]{1,0:T(1,128)} %bitcast.38, bf16[2048,128]{1,0:T(8,128)(2,1)} %wq_ref.3, ...), custom_call_target="tpu_custom_call" | custom-call | flops 12000000000 | bytes 30000000 | tf_op jit(solution)/shard_map/back/pallas_call | solution.py:464
  377.5 113.2 %ring_3.1 = (bf16[16,2,4,16,2048]{4,3,2,1,0:T(8,128)(2,1)}, f32[2,2048]{1,0:T(2,128)}, f32[16,2,64,256]{3,2,1,0:T(8,128)}) custom-call(bf16[16,2,4,16,2048]{4,3,2,1,0:T(8,128)(2,1)} %bitcast.41, bf16[2,4,16,2048]{3,2,1,0:T(8,128)(2,1)} %bitcast.26, f32[2,4,16,2048]{3,2,1,0:T(8,128)} %get-tuple-element.40.refs_2_, f32[1,2048]{1,0:T(1,128)} %bitcast.39, ...), custom_call_target="tpu_custom_call" | custom-call | flops 80000000000 | bytes 16777216 | tf_op jit(solution)/shard_map/ring_3/pallas_call | solution.py:333
  490.7 1.4 fusion.1
  492.1 3.0 fusion
  495.1 8.4 %copy.25 = bf16[2,1024,2048]{2,1,0:T(8,128)(2,1)} copy(bf16[2,1024,2048]{2,1,0:T(8,128)(2,1)} %bitcast.22) | data formatting | bytes 16777216
  503.6 8.4 %copy.26 = bf16[2,1024,2048]{2,1,0:T(8,128)(2,1)} copy(bf16[2,1024,2048]{2,1,0:T(8,128)(2,1)} %bitcast.23) | data formatting | bytes 16777216

commit v2 on v1

--- a/solution.py
+++ b/solution.py
@@ -241,23 +241,6 @@
     pltpu.make_async_copy(gat, gat, wo_sem).wait()
 
 
-class ForwardTail:
-    @staticmethod
-    def begin(ins, outs):
-        return None
-
-    @staticmethod
-    def piece(v, d, j, ins, outs, state):
-        h = (ins[0][d, j].astype(F32) + v).astype(BF)
-        outs[0][d, j] = h
-        normed, _ = rms_parts(h)
-        return (normed * ins[1][...]).astype(BF), state
-
-    @staticmethod
-    def end(outs, state):
-        pass
-
-
 class AddTail:
     @staticmethod
     def begin(ins, outs):
@@ -270,24 +253,6 @@
     @staticmethod
     def end(outs, state):
         pass
-
-
-class MlpTail:
-    @staticmethod
-    def begin(ins, outs):
-        return jnp.zeros(ins[2].shape, F32)
-
-    @staticmethod
-    def piece(v, d, j, ins, outs, state):
-        normed, inv = rms_parts(ins[0][d, j])
-        state = state + jnp.sum(v * normed, axis=0, keepdims=True)
-        grad = ins[1][d, j].astype(F32) + rms_back(v, normed, inv, ins[2][...])
-        outs[0][d, j] = grad
-        return grad.astype(BF), state
-
-    @staticmethod
-    def end(outs, state):
-        outs[1][...] = state
 
 
 class AttnTail:
@@ -403,10 +368,12 @@
 
 
 def back_kernel(dr_ref, x_ref, sg_ref, g_ref, wq_ref, wk_ref, wv_ref, wo_ref, q_ref, qkv_ref, ctx_ref,
-                ga_ref, dwq_ref, dkv_ref, dwo_ref, dqkv_s, dk_s, dv_s, w_ref):
+                y_in, dg_in, du_in, dd_in, ga_ref, dwq_ref, dkv_ref, dwo_ref, y_ref, dg_ref, du_ref, dd_ref, dqkv_s, dk_s, dv_s, w_ref):
     b, ph = pl.program_id(0), pl.program_id(1)
     nq = pl.num_programs(1) // 2
     scale = HEAD_DIM ** -0.5
+    for src, dst in ((y_in, y_ref), (dg_in, dg_ref), (du_in, du_ref), (dd_in, dd_ref)):
+        dst[...] = src[...]
 
     @pl.when((ph == 0) & (b == 0))
     def _():
@@ -453,7 +420,7 @@
         ga_ref[0] = mm_nt(blk, w_ref[...]).astype(BF)
 
 
-def back_call(dr, x, seg, gain, w_q, w_k, w_v, w_o, qkv, ctx):
+def back_call(dr, x, seg, gain, w_q, w_k, w_v, w_o, qkv, ctx, carried):
     nb, seq, width = x.shape
     nq = seq // BLK
     e3 = 3 * HEAD_DIM
@@ -461,62 +428,305 @@
     second = lambda n: pl.BlockSpec((1, BLK, n), lambda b, i: (b, jnp.maximum(i - nq, 0), 0))
     whole = lambda arr: pl.BlockSpec(arr.shape, lambda b, i: (0, 0))
     const = lambda shp: pl.BlockSpec(shp, lambda b, i: (0, 0))
+    n_steps = nb * 2 * nq
+    y, grads = carried[0], carried[1:]
+    thru = [pl.BlockSpec((y.shape[0] // n_steps, width), lambda b, i: (b * 2 * nq + i, 0))]
+    thru += [pl.BlockSpec((g.shape[0], width // n_steps), lambda b, i: (0, b * 2 * nq + i)) for g in grads]
     return pl.pallas_call(
         back_kernel,
         grid=(nb, 2 * nq),
         in_specs=[first(width), second(width), whole(seg), whole(gain), whole(w_q), whole(w_k), whole(w_v), whole(w_o),
-                  first(HEAD_DIM), pl.BlockSpec((1, seq, e3), lambda b, i: (b, 0, 0)), first(HEAD_DIM)],
-        out_specs=[second(width), const((width, HEAD_DIM)), const((width, 2 * HEAD_DIM)), const((HEAD_DIM, width))],
+                  first(HEAD_DIM), pl.BlockSpec((1, seq, e3), lambda b, i: (b, 0, 0)), first(HEAD_DIM)] + thru,
+        out_specs=[second(width), const((width, HEAD_DIM)), const((width, 2 * HEAD_DIM)), const((HEAD_DIM, width))] + thru,
         out_shape=[jax.ShapeDtypeStruct((nb, seq, width), BF), jax.ShapeDtypeStruct((width, HEAD_DIM), F32),
                    jax.ShapeDtypeStruct((width, 2 * HEAD_DIM), F32),
-                   jax.ShapeDtypeStruct((HEAD_DIM, width), F32)],
+                   jax.ShapeDtypeStruct((HEAD_DIM, width), F32)] + [jax.ShapeDtypeStruct(c.shape, c.dtype) for c in carried],
         scratch_shapes=[pltpu.VMEM((seq, e3), BF), pltpu.VMEM((seq, HEAD_DIM), F32), pltpu.VMEM((seq, HEAD_DIM), F32), pltpu.VMEM((width, e3), BF)],
         name='back',
         compiler_params=pltpu.CompilerParams(vmem_limit_bytes=VMEM_LIMIT),
         cost_estimate=pl.CostEstimate(flops=12_000_000_000, bytes_accessed=30_000_000, transcendentals=0),
-    )(dr, x, seg, gain, w_q, w_k, w_v, w_o, qkv, qkv, ctx)
-
-
-def mlp_kernel(m_ref, dy_ref, wg_ref, wu_ref, wd_ref, p_ref, gm_ref, dwg_ref, dwu_ref, dwd_ref):
-    @pl.when(pl.program_id(0) == 0)
-    def _():
-        dwg_ref[...] = jnp.zeros_like(dwg_ref)
-        dwu_ref[...] = jnp.zeros_like(dwu_ref)
-        dwd_ref[...] = jnp.zeros_like(dwd_ref)
-
-    m = m_ref[...]
-    dy = dy_ref[...]
-    gate = mm_nt(m, wg_ref[...])
-    upper = mm_nt(m, wu_ref[...])
-    sig = jax.nn.sigmoid(gate)
-    act = (gate * sig * upper).astype(BF)
-    p_ref[...] = mm(act, wd_ref[...]).astype(BF)
-    dact = mm_nt(dy, wd_ref[...])
-    dwd_ref[...] += mm_tn(act, dy)
-    dgate = (dact * upper * sig * (1.0 + gate * (1.0 - sig))).astype(BF)
-    dupper = (dact * gate * sig).astype(BF)
-    dwg_ref[...] += mm_tn(dgate, m)
-    dwu_ref[...] += mm_tn(dupper, m)
-    gm_ref[...] = (mm(dgate, wg_ref[...]) + mm(dupper, wu_ref[...])).astype(BF)
-
-
-def mlp_call(m, dy, w_gate, w_up, w_down):
-    tokens, width = m.shape
+    )(dr, x, seg, gain, w_q, w_k, w_v, w_o, qkv, qkv, ctx, *carried)
+
+
+def mid_kernel(chips, part, x, dy, g_ref, wg, wu, wd, out, p_out, h_own, x_own, dres_own, gpart, dwg, dwu, dwd,
+               loc, oth, arr, gat, gat2, dyb, pst, gst, dy_own,
+               ld_sem, xs_sem, xr_sem, rs_sem, rr_sem, as_sem, ar_sem, ps_sem, pm_sem, own_sem, dy_sem, po_sem,
+               xs2_sem, xr2_sem, rs2_sem, rr2_sem, as2_sem, ar2_sem, ps2_sem, pr2_sem, wo_sem):
+    me = lax.axis_index('tp')
+    chip = me // 2
+    core = me % 2
+    mate = chip * 2 + 1 - core
+    nxt = (lax.rem(chip + 1, chips) * 2 + core, lax.rem(chip + chips - 1, chips) * 2 + core)
+    width = x.shape[-1]
+    last = chips - 1
+
+    def remote(src, dst, ssem, rsem, t):
+        return pltpu.make_async_remote_copy(src_ref=src, dst_ref=dst, send_sem=ssem, recv_sem=rsem,
+                                            device_id={'tp': t}, device_id_type=MESH)
+
+    barrier = pltpu.get_barrier_semaphore()
+    for t in (nxt[0], nxt[1], mate):
+        pl.semaphore_signal(barrier, inc=1, device_id={'tp': t}, device_id_type=MESH)
+    pl.semaphore_wait(barrier, 3)
+
+    def chunk_at(d, s):
+        return lax.rem(chip + (s if d == 1 else chips - s), chips)
+
+    def swap(d, s):
+        m = chunk_at(d, s)
+        return remote(part.at[m * 2 + 1 - core, d], oth.at[m, d], xs_sem, xr_sem.at[m, d], mate)
+
+    def load(d, s):
+        m = chunk_at(d, s)
+        return pltpu.make_async_copy(part.at[m * 2 + core, d], loc.at[m, d], ld_sem.at[m, d])
+
+    def dy_copy(d, t):
+        m = chunk_at(d, t)
+        return pltpu.make_async_copy(dy.at[pl.ds(m * 2, 2), d], dyb.at[t % 2, d], dy_sem.at[t % 2, d])
+
+    for s in range(1, chips + 1):
+        for d in range(2):
+            swap(d, s % chips).start()
+            load(d, s % chips).start()
+    x_load = pltpu.make_async_copy(x.at[me], x_own, own_sem.at[0])
+    dy_load = pltpu.make_async_copy(dy.at[me], dy_own, own_sem.at[1])
+    x_load.start()
+    dy_load.start()
+    for d in range(2):
+        dy_copy(d, 0).start()
+    for acc in (dwg, dwu, dwd):
+        acc[...] = jnp.zeros_like(acc)
+
+    def rs_copy(d, j, s, m, ssem, rsem):
+        return remote(loc.at[m, d, j], arr.at[s, d, j], ssem, rsem.at[s, d, j], nxt[d])
+
+    def rs_step(s, first):
+        for d in range(2):
+            load(d, s + 1).wait()
+            swap(d, s + 1).wait_recv()
+        for j in range(SUB):
+            for d in range(2):
+                m = chunk_at(d, s + 1)
+                v = loc[m, d, j].astype(F32) + oth[m, d, j].astype(F32)
+                if not first:
+                    rs_copy(d, j, s - 1, m, rs_sem, rr_sem).wait_recv()
+                    v = v + arr[s - 1, d, j].astype(F32)
+                loc[m, d, j] = v.astype(BF)
+                rs_copy(d, j, s, m, rs_sem, rr_sem).start()
+
+    rs_step(0, True)
+
+    @pl.loop(1, last)
+    def _(s):
+        rs_step(s, False)
+
+    def ag_copy(d, j, t, m):
+        return remote(gat.at[m * 2 + core, d, j], gat.at[m * 2 + core, d, j], as_sem, ar_sem.at[t, d, j], nxt[d])
+
+    def spread(d, j, t, m):
+        remote(gat.at[m * 2 + core, d, j], gat.at[m * 2 + core, d, j], ps_sem, pm_sem.at[t], mate).start()
+
+    x_load.wait()
+    dy_load.wait()
+    for d in range(2):
+        load(d, 0).wait()
+        swap(d, 0).wait_recv()
+    for j in range(SUB):
+        for d in range(2):
+            rs_copy(d, j, last - 1, chip, rs_sem, rr_sem).wait_recv()
+            v = loc[chip, d, j].astype(F32) + oth[chip, d, j].astype(F32) + arr[last - 1, d, j].astype(F32)
+            h = (x_own[d, j].astype(F32) + v.astype(BF).astype(F32)).astype(BF)
+            h_own[d, j] = h
+            normed, _ = rms_parts(h)
+            gat[me, d, j] = (normed * g_ref[...]).astype(BF)
+            ag_copy(d, j, 0, chip).start()
+            spread(d, j, 0, chip)
+
+    def bulk(ref, sem, rsem):
+        return remote(ref, ref, sem, rsem, mate)
+
+    bulk(arr, rs_sem, pr2_sem).wait_send()
+
+    def p_copy(d, t):
+        m = chunk_at(d, t)
+        return pltpu.make_async_copy(pst.at[t % 2, d], p_out.at[pl.ds(m * 2, 2), d], po_sem.at[t % 2, d])
+
+    def swap2(d, t):
+        m = chunk_at(d, t)
+        return remote(gst.at[t % 2, d, 1 - core], oth.at[m, d], xs2_sem.at[t % 2, d], xr2_sem.at[m, d], mate)
+
+    def rs2_step(t, first):
+        slot = t % 2
+        for d in range(2):
+            swap2(d, t).wait_recv()
+        for j in range(SUB):
+            for d in range(2):
+                m = chunk_at(d, t)
+                v = gst[slot, d, core, j].astype(F32) + oth[m, d, j].astype(F32)
+                if not first:
+                    rs_copy(d, j, t - 2, m, rs2_sem, rr2_sem).wait_recv()
+                    v = v + arr[t - 2, d, j].astype(F32)
+                loc[m, d, j] = v.astype(BF)
+                rs_copy(d, j, t - 1, m, rs2_sem, rr2_sem).start()
+
+    def collect(t, onward):
+        for j in range(SUB):
+            for d in range(2):
+                m = chunk_at(d, t)
+                ag_copy(d, j, t - 1, m).wait_recv()
+                if onward:
+                    ag_copy(d, j, t, m).start()
+                spread(d, j, t, m)
+
+    step = width // 4
+
+    @pl.loop(0, chips)
+    def _(t):
+        slot = t % 2
+        a = chunk_at(0, t)
+        b = chunk_at(1, t)
+
+        @pl.when((t > 0) & (t < last))
+        def _():
+            collect(t, True)
+
+        @pl.when(t == last)
+        def _():
+            collect(t, False)
+
+        @pl.when(t < last)
+        def _():
+            for d in range(2):
+                dy_copy(d, t + 1).start()
+
+        @pl.when(t >= 2)
+        def _():
+            for d in range(2):
+                p_copy(d, t - 2).wait()
+                swap2(d, t - 2).wait_send()
+
+        for d in range(2):
+            dy_copy(d, t).wait()
+        bulk(gat.at[0], ps_sem, pm_sem.at[t]).wait_recv()
+
+        rows = 4 * SUB * ROWS
+        mb = jnp.concatenate([gat[pl.ds(a * 2, 2), 0].reshape(rows // 2, width), gat[pl.ds(b * 2, 2), 1].reshape(rows // 2, width)], axis=0)
+        dyv = dyb[slot].reshape(rows, width)
+        gate = mm_nt(mb, wg[...])
+        upper = mm_nt(mb, wu[...])
+        dact = mm_nt(dyv, wd[...])
+        sig = jax.nn.sigmoid(gate)
+        act = (gate * sig * upper).astype(BF)
+        dgate = (dact * upper * sig * (1.0 + gate * (1.0 - sig))).astype(BF)
+        dupper = (dact * gate * sig).astype(BF)
+        for n in range(4):
+            cs = slice(n * step, (n + 1) * step)
+            gst[slot, :, :, :, :, cs] = (mm(dgate, wg[:, cs]) + mm(dupper, wu[:, cs])).astype(BF).reshape(2, 2, SUB, ROWS, step)
+        for d in range(2):
+            swap2(d, t).start()
+        for n in range(4):
+            cs = slice(n * step, (n + 1) * step)
+            pst[slot, :, :, :, :, cs] = mm(act, wd[:, cs]).astype(BF).reshape(2, 2, SUB, ROWS, step)
+            dwd[:, cs] += mm_tn(act, dyv[:, cs])
+            dwg[:, cs] += mm_tn(dgate, mb[:, cs])
+            dwu[:, cs] += mm_tn(dupper, mb[:, cs])
+        for d in range(2):
+            p_copy(d, t).start()
+
+        @pl.when(t == 0)
+        def _():
+            for d in range(2):
+                loc[chip, d] = gst[0, d, core]
+
+        @pl.when(t == 1)
+        def _():
+            rs2_step(t, True)
+
+        @pl.when(t > 1)
+        def _():
+            rs2_step(t, False)
+
+    def ag2_copy(d, j, t, m):
+        return remote(gat2.at[m, d, j], gat2.at[m, d, j], as2_sem, ar2_sem.at[t, d, j], nxt[d])
+
+    def spread2(d, j, m):
+        remote(gat2.at[m, d, j], out.at[m * 2 + core, d, j], ps2_sem, pr2_sem, mate).start()
+        pltpu.make_async_copy(gat2.at[m, d, j], out.at[m * 2 + core, d, j], wo_sem).start()
+
+    for d in range(2):
+        swap2(d, 0).wait_recv()
+    total = jnp.zeros((1, width), F32)
+    for j in range(SUB):
+        for d in range(2):
+            rs_copy(d, j, last - 1, chip, rs2_sem, rr2_sem).wait_recv()
+            v = loc[chip, d, j].astype(F32) + oth[chip, d, j].astype(F32) + arr[last - 1, d, j].astype(F32)
+            v = v.astype(BF).astype(F32)
+            normed, inv = rms_parts(h_own[d, j])
+            total = total + jnp.sum(v * normed, axis=0, keepdims=True)
+            grad = dy_own[d, j].astype(F32) + rms_back(v, normed, inv, g_ref[...])
+            dres_own[d, j] = grad
+            gat2[chip, d, j] = grad.astype(BF)
+            ag2_copy(d, j, 0, chip).start()
+            spread2(d, j, chip)
+    gpart[...] = total
+
+    def ag2_step(t, onward):
+        for j in range(SUB):
+            for d in range(2):
+                m = chunk_at(d, t)
+                ag2_copy(d, j, t - 1, m).wait_recv()
+                if onward:
+                    ag2_copy(d, j, t, m).start()
+                spread2(d, j, m)
+
+    @pl.loop(1, last)
+    def _(t):
+        ag2_step(t, True)
+
+    ag2_step(last, False)
+
+    bulk(gat2, ps2_sem, pr2_sem).wait_recv()
+    for sem in (xs_sem, ps_sem, ps2_sem):
+        bulk(oth, sem, pr2_sem).wait_send()
+    for sem in (as_sem, rs2_sem, as2_sem):
+        bulk(arr, sem, pr2_sem).wait_send()
+    for t in (chips - 2, chips - 1):
+        for d in range(2):
+            p_copy(d, t).wait()
+            swap2(d, t).wait_send()
+    pltpu.make_async_copy(gat2, gat2, wo_sem).wait()
+
+
+def mid_call(part, x, dy, gain, w_gate, w_up, w_down, chips, cid):
+    tokens, width = part.shape
     ff = w_down.shape[0]
-    rowblk = pl.BlockSpec((BLK, width), lambda i: (i, 0))
-    const = lambda shp: pl.BlockSpec(shp, lambda i: (0, 0))
-    return pl.pallas_call(
-        mlp_kernel,
-        grid=(tokens // BLK,),
-        in_specs=[rowblk, rowblk, const((ff, width)), const((ff, width)), const((ff, width))],
-        out_specs=[rowblk, rowblk, const((ff, width)), const((ff, width)), const((ff, width))],
-        out_shape=[jax.ShapeDtypeStruct((tokens, width), BF), jax.ShapeDtypeStruct((tokens, width), BF),
-                   jax.ShapeDtypeStruct((ff, width), F32), jax.ShapeDtypeStruct((ff, width), F32),
-                   jax.ShapeDtypeStruct((ff, width), F32)],
-        name='mlp',
-        compiler_params=pltpu.CompilerParams(vmem_limit_bytes=VMEM_LIMIT),
-        cost_estimate=pl.CostEstimate(flops=32_000_000_000, bytes_accessed=50_000_000, transcendentals=0),
-    )(m, dy, w_gate, w_up, w_down)
+    shape = (chips * 2, 2, SUB, ROWS, width)
+    half = (chips, 2, SUB, ROWS, width)
+    arrive = (chips - 1, 2, SUB, ROWS, width)
+    piece = (2, SUB, ROWS, width)
+    pair = (2, 2, 2, SUB, ROWS, width)
+    vm = pl.BlockSpec(memory_space=pltpu.VMEM)
+    anyspec = pl.BlockSpec(memory_space=pl.ANY)
+    dma = pltpu.SemaphoreType.DMA
+    steps = dma((chips - 1, 2, SUB))
+    vmb = lambda shp: pltpu.VMEM(shp, BF)
+    grad = jax.ShapeDtypeStruct((ff, width), F32)
+    res = pl.pallas_call(
+        functools.partial(mid_kernel, chips),
+        out_shape=[jax.ShapeDtypeStruct(shape, BF), jax.ShapeDtypeStruct(shape, BF), jax.ShapeDtypeStruct(piece, BF),
+                   jax.ShapeDtypeStruct(piece, BF), jax.ShapeDtypeStruct(piece, F32), jax.ShapeDtypeStruct((1, width), F32),
+                   grad, grad, grad],
+        in_specs=[anyspec] * 3 + [vm] * 4,
+        out_specs=[anyspec] * 2 + [vm] * 7,
+        scratch_shapes=[
+            vmb(half), vmb(half), vmb(arrive), vmb(shape), vmb(half), vmb(pair), vmb(pair), vmb(pair), vmb(piece),
+            dma((chips, 2)), dma, dma((chips, 2)), dma, steps, dma, steps, dma, dma((chips,)), dma((2,)), dma((2, 2)), dma((2, 2)),
+            dma((2, 2)), dma((chips, 2)), dma, steps, dma, steps, dma, dma, dma],
+        name='middle',
+        compiler_params=pltpu.CompilerParams(collective_id=cid, has_side_effects=True, vmem_limit_bytes=67_000_000),
+        cost_estimate=pl.CostEstimate(flops=120_000_000_000, bytes_accessed=40 * tokens * width, transcendentals=0),
+    )(part.reshape(shape), x.reshape(shape), dy.reshape(shape), gain, w_gate, w_up, w_down)
+    return (res[0].reshape(tokens, width), res[1].reshape(tokens, width)) + tuple(res[2:])
 
 
 def solution(mesh):
@@ -527,27 +737,16 @@
         nb, seq, width = hidden.shape
         tokens = nb * seq
         own = tokens // tp_size
-        row0 = lax.axis_index('tp') * own
-        piece = (2, SUB, ROWS, width)
-
-        def own_rows(arr):
-            return lax.dynamic_slice_in_dim(arr.reshape(tokens, width), row0, own, axis=0).reshape(piece)
-
         g1 = gain_attn[None, :]
         g2 = gain_mlp[None, :]
-        x_own = own_rows(hidden)
-        dy_own = own_rows(grad_out)
-        shard_bf = jax.ShapeDtypeStruct(piece, BF)
-        shard_f = jax.ShapeDtypeStruct(piece, F32)
-        gain_f = jax.ShapeDtypeStruct((1, width), F32)
         weights = (w_q, w_k, w_v, w_o)
 
         o_part, qkv, ctx = front_call(hidden, seg_ids, g1, *weights)
-        mixed, h_own = ring_call(o_part.reshape(tokens, width), [x_own, g2], [shard_bf], ForwardTail, chips, 1)
-        p_part, gm_part, d_gate, d_up, d_down = mlp_call(mixed, grad_out.reshape(tokens, width), w_gate.T, w_up.T, w_down)
-        dres, dres_own, g2_part = ring_call(gm_part, [h_own, dy_own, g2], [shard_f, gain_f], MlpTail, chips, 2)
-        ga_part, d_q, d_kv, d_o = back_call(dres.reshape(nb, seq, width), hidden, seg_ids, g1, *weights, qkv, ctx)
+        dres, p_part, h_own, x_own, dres_own, g2_part, d_gate, d_up, d_down = mid_call(
+            o_part.reshape(tokens, width), hidden, grad_out, g2, w_gate.T, w_up.T, w_down, chips, 1)
         (y_out,) = ring_call(p_part, [h_own], [], AddTail, chips, 4)
+        ga_part, d_q, d_kv, d_o, y_out, d_gate, d_up, d_down = back_call(
+            dres.reshape(nb, seq, width), hidden, seg_ids, g1, *weights, qkv, ctx, (y_out, d_gate, d_up, d_down))
         kv_rows = own // 2
         kv_shape = (tp_size, 2, kv_rows, 2 * HEAD_DIM)
         dx, gains, d_kv = ring_call(ga_part.reshape(tokens, width), [x_own, dres_own, g1, g1, g2_part, d_kv.reshape(kv_shape)],

time: 512 us -> 464 us (0.906)
  Pallas kernels: 488 us -> 450 us
  local copies, waits for them, and re-layouts: 23.6 us -> 12.8 us
    pallas_call x4 -> x2, Pallas kernels: 385 us -> 201 us  [ring_call(): pl.pallas_call(body, out_shape=[jax.ShapeDtypeStruct(shape, BF)] + out_sh...]
    pallas_call x1, Pallas kernels: 46.6 us -> 189 us  [mid_call(): pl.pallas_call(functools.partial(mid_kernel, chips), out_shape=[jax.Shape...]
    unnamed x2 -> x1, local copies, waits for them, and re-layouts: 16.9 us -> 8.44 us
where the time goes in v2:
time: 464 us
  Pallas kernels  450 us (97%)
  local copies, waits for them, and re-layouts  12.8 us (3%)
    pallas_call x2, Pallas kernels, ring_call(): pl.pallas_call(body, out_shape=[jax.ShapeDtypeStruct(shape, BF)] + out_sh...  201 us
    pallas_call x1, Pallas kernels, mid_call(): pl.pallas_call(functools.partial(mid_kernel, chips), out_shape=[jax.Shape...  189 us
    pallas_call x1, Pallas kernels, back_call(): pl.pallas_call(back_kernel, grid=(nb, 2 * nq), in_specs=[first(width), se...  39.7 us
    pallas_call x1, Pallas kernels, front_call(): pl.pallas_call(front_kernel, grid=(nb, seq // BLK), in_specs=[rowblk(widt...  20.8 us

profile of v2, /device:TPU:21, one launch (start us, length us, event | category | flops | bytes accessed | tf_op | source)
XLA Modules:
  0.0 463.8 jit_solution(9241093866998819634)
XLA Ops:
  0.6 20.8 %front.1 = (bf16[2,1024,2048]{2,1,0:T(8,128)(2,1)}, bf16[2,1024,384]{2,1,0:T(8,128)(2,1)}, bf16[2,1024,128]{2,1,0:T(8,128)(2,1)}) custom-call(bf16[2,1024,2048]{2,1,0:T(8,128)(2,1)} %x_ref.3, s32[2,1024]{1,0:T(2,128)} %sg_ref.3, f32[1,2048]{1,0:T(1,128)} %bitcast.27, bf16[2048,128]{1,0:T(8,128)(2,1)} %wq_ref.3, bf16[2048,128]{1,0:T(8,128)(2,1)} %wk_ref.3, ...), custom_call_target="tpu_custom_call" | custom-call | flops 8000000000 | bytes 20000000 | tf_op jit(solution)/shard_map/front/pallas_call | solution.py:356
  21.4 188.5 %middle.1 = (bf16[16,2,4,16,2048]{4,3,2,1,0:T(8,128)(2,1)}, bf16[16,2,4,16,2048]{4,3,2,1,0:T(8,128)(2,1)}, bf16[2,4,16,2048]{3,2,1,0:T(8,128)(2,1)}, bf16[2,4,16...) custom-call(bf16[16,2,4,16,2048]{4,3,2,1,0:T(8,128)(2,1)} %bitcast.3, ...), custom_call_target="tpu_custom_call" | custom-call | flops 120000004096 | bytes 167772160 | tf_op jit(solution)/shard_map/middle/pallas_call | solution.py:714
  210.0 88.1 %ring_4.1 = bf16[16,2,4,16,2048]{4,3,2,1,0:T(8,128)(2,1)} custom-call(bf16[16,2,4,16,2048]{4,3,2,1,0:T(8,128)(2,1)} %get-tuple-element.38.refs_0_, bf16[2,4,16,2048]{3,2,1,0:T(8,128)(2,1)} %get-tuple-element.39.refs_1_), custom_call_target="tpu_custom_call" | custom-call | flops 80000000000 | bytes 16777216 | tf_op jit(solution)/shard_map/ring_4/pallas_call | solution.py:298
  298.1 39.7 %back.1 = (bf16[2,1024,2048]{2,1,0:T(8,128)(2,1)}, f32[2048,128]{1,0:T(8,128)}, f32[2048,256]{1,0:T(8,128)}, f32[128,2048]{1,0:T(8,128)}, bf16[2048,2048]{1,0:T(...) custom-call(bf16[2,1024,2048]{2,1,0:T(8,128)(2,1)} %bitcast.32, ...), custom_call_target="tpu_custom_call" | custom-call | flops 12000000000 | bytes 30000000 | tf_op jit(solution)/shard_map/back/pallas_call | solution.py:435
  337.8 113.2 %ring_3.1 = (bf16[16,2,4,16,2048]{4,3,2,1,0:T(8,128)(2,1)}, f32[2,2048]{1,0:T(2,128)}, f32[16,2,64,256]{3,2,1,0:T(8,128)}) custom-call(bf16[16,2,4,16,2048]{4,3,2,1,0:T(8,128)(2,1)} %bitcast.33, bf16[2,4,16,2048]{3,2,1,0:T(8,128)(2,1)} %get-tuple-element.45.refs_1_, f32[2,4,16,2048]{3,2,1,0:T(8,128)} %get-tuple-element.46.refs_2_, f32[1,2048]{1,0:T(1,128)} %bitcast.29, ...), custom_call_target="tpu_custom_call" | custom-call | flops 80000000000 | bytes 16777216 | tf_op jit(solution)/shard_map/ring_3/pallas_call | solution.py:298
  451.0 1.4 fusion.1
  452.4 3.0 fusion
  455.4 8.4 %copy.24 = bf16[2,1024,2048]{2,1,0:T(8,128)(2,1)} copy(bf16[2,1024,2048]{2,1,0:T(8,128)(2,1)} %bitcast.18) | data formatting | bytes 16777216

commit v3 on v2

--- a/solution.py
+++ b/solution.py
@@ -40,7 +40,7 @@
     return inv * (scaled - normed * jnp.mean(scaled * normed, axis=-1, keepdims=True))
 
 
-def ring_kernel(chips, n_in, n_out, epilogue, with_gain, part, *refs):
+def ring_kernel(chips, n_in, n_out, epilogue, with_gain, task, part, *refs):
     ins = refs[:n_in]
     out = refs[n_in]
     outs = refs[n_in + 1:n_in + 1 + n_out]
@@ -140,9 +140,18 @@
 
     rs_step(0, True)
 
+    if task:
+        work, work_end, work_count = task(ins, outs, scratch[14:])
+
+    def work_share(n):
+        if task:
+            span = 2 * (chips - 2)
+            pl.loop(n * work_count // span, (n + 1) * work_count // span)(work)
+
     @pl.loop(1, chips - 1)
     def _(s):
         rs_step(s, False)
+        work_share(s - 1)
 
     def ag_copy(d, j, t, m):
         return pltpu.make_async_remote_copy(
@@ -207,8 +216,11 @@
     @pl.loop(1, chips - 1)
     def _(t):
         ag_step(t, False)
+        work_share(chips - 3 + t)
 
     ag_step(chips - 1, True)
+    if task:
+        work_end()
 
     if with_gain:
         tot = gacc[...]
@@ -272,7 +284,7 @@
         pass
 
 
-def ring_call(part, ins, out_shapes, epilogue, chips, cid, with_gain=False):
+def ring_call(part, ins, out_shapes, epilogue, chips, cid, with_gain=False, task=None, in_any=(), out_any=(), extra=()):
     tokens, width = part.shape
     shape = (chips * 2, 2, SUB, ROWS, width)
     half = (chips, 2, SUB, ROWS, width)
@@ -290,16 +302,17 @@
         kshape = ins[5].shape[1:]
         scratch += [pltpu.VMEM((chips,) + kshape, F32), pltpu.VMEM((chips,) + kshape, F32), pltpu.VMEM((chips - 1,) + kshape, F32),
                     dma, dma((chips, 2)), dma, dma((chips - 1, 2)), dma, dma((chips - 1, 2)), dma, dma]
+    scratch += list(extra)
     n_in, n_out = len(ins), len(out_shapes)
 
     def body(*refs):
-        ring_kernel(chips, n_in, n_out, epilogue, with_gain, *refs)
+        ring_kernel(chips, n_in, n_out, epilogue, with_gain, task, *refs)
 
     res = pl.pallas_call(
         body,
         out_shape=[jax.ShapeDtypeStruct(shape, BF)] + out_shapes,
-        in_specs=[anyspec] + [vm] * n_in,
-        out_specs=[anyspec] + [vm] * n_out,
+        in_specs=[anyspec] + [anyspec if n in in_any else vm for n in range(n_in)],
+        out_specs=[anyspec] + [anyspec if n in out_any else vm for n in range(n_out)],
         scratch_shapes=scratch,
         name='ring_%d' % cid,
         compiler_params=pltpu.CompilerParams(collective_id=cid, has_side_effects=True, vmem_limit_bytes=VMEM_LIMIT),
@@ -367,85 +380,131 @@
     )(x, seg, gain, w_q, w_k, w_v, w_o)
 
 
-def back_kernel(dr_ref, x_ref, sg_ref, g_ref, wq_ref, wk_ref, wv_ref, wo_ref, q_ref, qkv_ref, ctx_ref,
-                y_in, dg_in, du_in, dd_in, ga_ref, dwq_ref, dkv_ref, dwo_ref, y_ref, dg_ref, du_ref, dd_ref, dqkv_s, dk_s, dv_s, w_ref):
-    b, ph = pl.program_id(0), pl.program_id(1)
-    nq = pl.num_programs(1) // 2
+def back_task(ins, outs, scratch):
+    dr_ref, x_ref, sg_ref, g_ref, wq_ref, wk_ref, wv_ref, wo_ref, qkv_ref, ctx_ref = ins[1:]
+    ga_ref, dwq_ref, dkv_ref, dwo_ref = outs
+    inb, gab, dqkv_s, dk_s, dv_s, w_ref, in_sem, ga_sem = scratch
+    nb, seq, width = dr_ref.shape
+    nq = seq // BLK
+    count = nb * 2 * nq
     scale = HEAD_DIM ** -0.5
-    for src, dst in ((y_in, y_ref), (dg_in, dg_ref), (du_in, du_ref), (dd_in, dd_ref)):
-        dst[...] = src[...]
-
-    @pl.when((ph == 0) & (b == 0))
-    def _():
-        pack(w_ref, wq_ref, wk_ref, wv_ref)
-        dwq_ref[...] = jnp.zeros_like(dwq_ref)
-        dkv_ref[...] = jnp.zeros_like(dkv_ref)
-        dwo_ref[...] = jnp.zeros_like(dwo_ref)
-
-    @pl.when(ph == 0)
-    def _():
-        dk_s[...] = jnp.zeros_like(dk_s)
-        dv_s[...] = jnp.zeros_like(dv_s)
-
-    @pl.when(ph < nq)
-    def _():
-        row0 = pl.multiple_of(ph * BLK, BLK)
-        dr = dr_ref[0]
-        dctx = mm_nt(dr, wo_ref[...]).astype(BF)
-        dwo_ref[...] += mm_tn(ctx_ref[0], dr)
-        q = q_ref[0]
-        k = qkv_ref[0, :, HEAD_DIM:2 * HEAD_DIM]
-        v = qkv_ref[0, :, 2 * HEAD_DIM:]
-        probs = masked_probs(q, k, sg_ref, b, row0)
-        dp = mm_nt(dctx, v)
-        ds = (probs * (dp - jnp.sum(dp * probs, axis=-1, keepdims=True)) * scale).astype(BF)
-        dv_s[...] += mm_tn(probs.astype(BF), dctx)
-        dk_s[...] += mm_tn(ds, q)
-        dqkv_s[pl.ds(row0, BLK), :HEAD_DIM] = mm(ds, k).astype(BF)
-
-    @pl.when(ph == nq - 1)
-    def _():
-        dqkv_s[:, HEAD_DIM:2 * HEAD_DIM] = dk_s[...].astype(BF)
-        dqkv_s[:, 2 * HEAD_DIM:] = dv_s[...].astype(BF)
-
-    @pl.when(ph >= nq)
-    def _():
-        row0 = pl.multiple_of((ph - nq) * BLK, BLK)
-        normed, _ = rms_parts(x_ref[0])
-        a = (normed * g_ref[...]).astype(BF)
-        blk = dqkv_s[pl.ds(row0, BLK)]
-        dw = mm_tn(a, blk)
-        dwq_ref[...] += dw[:, :HEAD_DIM]
-        dkv_ref[...] += dw[:, HEAD_DIM:]
-        ga_ref[0] = mm_nt(blk, w_ref[...]).astype(BF)
-
-
-def back_call(dr, x, seg, gain, w_q, w_k, w_v, w_o, qkv, ctx, carried):
-    nb, seq, width = x.shape
-    nq = seq // BLK
-    e3 = 3 * HEAD_DIM
-    first = lambda n: pl.BlockSpec((1, BLK, n), lambda b, i: (b, jnp.minimum(i, nq - 1), 0))
-    second = lambda n: pl.BlockSpec((1, BLK, n), lambda b, i: (b, jnp.maximum(i - nq, 0), 0))
-    whole = lambda arr: pl.BlockSpec(arr.shape, lambda b, i: (0, 0))
-    const = lambda shp: pl.BlockSpec(shp, lambda b, i: (0, 0))
-    n_steps = nb * 2 * nq
-    y, grads = carried[0], carried[1:]
-    thru = [pl.BlockSpec((y.shape[0] // n_steps, width), lambda b, i: (b * 2 * nq + i, 0))]
-    thru += [pl.BlockSpec((g.shape[0], width // n_steps), lambda b, i: (0, b * 2 * nq + i)) for g in grads]
+
+    def fetch(n):
+        b, ph = n // (2 * nq), n % (2 * nq)
+        row0 = pl.multiple_of((ph % nq) * BLK, BLK)
+
+        @pl.when(ph < nq)
+        def _():
+            pltpu.make_async_copy(dr_ref.at[b, pl.ds(row0, BLK)], inb.at[n % 2], in_sem.at[n % 2]).start()
+
+        @pl.when(ph >= nq)
+        def _():
+            pltpu.make_async_copy(x_ref.at[b, pl.ds(row0, BLK)], inb.at[n % 2], in_sem.at[n % 2]).start()
+
+    def ga_copy(b, i):
+        row0 = pl.multiple_of(i * BLK, BLK)
+        return pltpu.make_async_copy(gab.at[i % 2], ga_ref.at[b, pl.ds(row0, BLK)], ga_sem.at[i % 2])
+
+    pltpu.make_async_copy(dr_ref.at[0, pl.ds(0, BLK)], inb.at[0], in_sem.at[0]).start()
+    pack(w_ref, wq_ref, wk_ref, wv_ref)
+    dwq_ref[...] = jnp.zeros_like(dwq_ref)
+    dkv_ref[...] = jnp.zeros_like(dkv_ref)
+    dwo_ref[...] = jnp.zeros_like(dwo_ref)
+
+    def work(n):
+        b, ph = n // (2 * nq), n % (2 * nq)
+        row0 = pl.multiple_of((ph % nq) * BLK, BLK)
+
+        @pl.when(n + 1 < count)
+        def _():
+            fetch(n + 1)
+
+        pltpu.make_async_copy(dr_ref.at[0, pl.ds(0, BLK)], inb.at[n % 2], in_sem.at[n % 2]).wait()
+
+        @pl.when(ph == 0)
+        def _():
+            dk_s[...] = jnp.zeros_like(dk_s)
+            dv_s[...] = jnp.zeros_like(dv_s)
+
+        @pl.when(ph < nq)
+        def _():
+            dr = inb[n % 2]
+            dctx = mm_nt(dr, wo_ref[...]).astype(BF)
+            dwo_ref[...] += mm_tn(ctx_ref[b, pl.ds(row0, BLK)], dr)
+            q = qkv_ref[b, pl.ds(row0, BLK), :HEAD_DIM]
+            k = qkv_ref[b, :, HEAD_DIM:2 * HEAD_DIM]
+            v = qkv_ref[b, :, 2 * HEAD_DIM:]
+            probs = masked_probs(q, k, sg_ref, b, row0)
+            dp = mm_nt(dctx, v)
+            ds = (probs * (dp - jnp.sum(dp * probs, axis=-1, keepdims=True)) * scale).astype(BF)
+            dv_s[...] += mm_tn(probs.astype(BF), dctx)
+            dk_s[...] += mm_tn(ds, q)
+            dqkv_s[pl.ds(row0, BLK), :HEAD_DIM] = mm(ds, k).astype(BF)
+
+        @pl.when(ph == nq - 1)
+        def _():
+            dqkv_s[:, HEAD_DIM:2 * HEAD_DIM] = dk_s[...].astype(BF)
+            dqkv_s[:, 2 * HEAD_DIM:] = dv_s[...].astype(BF)
+
+        @pl.when(ph >= nq)
+        def _():
+            i = ph - nq
+            normed, _ = rms_parts(inb[n % 2])
+            a = (normed * g_ref[...]).astype(BF)
+            blk = dqkv_s[pl.ds(row0, BLK)]
+            dw = mm_tn(a, blk)
+            dwq_ref[...] += dw[:, :HEAD_DIM]
+            dkv_ref[...] += dw[:, HEAD_DIM:]
+
+            @pl.when((b > 0) | (i >= 2))
+            def _():
+                ga_copy(b, i).wait()
+
+            gab[i % 2] = mm_nt(blk, w_ref[...]).astype(BF)
+            ga_copy(b, i).start()
+
+    def end():
+        for i in (nq - 2, nq - 1):
+            ga_copy(nb - 1, i).wait()
+
+    return work, end, count
+
+
+def back_scratch(seq, width):
+    return [pltpu.VMEM((2, BLK, width), BF), pltpu.VMEM((2, BLK, width), BF), pltpu.VMEM((seq, 3 * HEAD_DIM), BF),
+            pltpu.VMEM((seq, HEAD_DIM), F32), pltpu.VMEM((seq, HEAD_DIM), F32), pltpu.VMEM((width, 3 * HEAD_DIM), BF),
+            pltpu.SemaphoreType.DMA((2,)), pltpu.SemaphoreType.DMA((2,))]
+
+
+def finish_kernel(n_copy, *refs):
+    ins, outs = refs[:n_copy + 2], refs[n_copy + 2:]
+    for n in range(n_copy):
+        outs[n][...] = ins[n][...]
+    kv, gains = ins[n_copy], ins[n_copy + 1]
+    for n in range(2):
+        outs[n_copy + n][...] = kv[:, n * HEAD_DIM:(n + 1) * HEAD_DIM]
+        outs[n_copy + 2 + n][...] = gains[n:n + 1, :]
+
+
+def finish_call(by_rows, by_cols, kv, gains):
+    steps = 16
+    rows = lambda a: pl.BlockSpec((a.shape[0] // steps, a.shape[1]), lambda i: (i, 0))
+    cols = lambda a: pl.BlockSpec((a.shape[0], a.shape[1] // steps), lambda i: (0, i))
+    half = jax.ShapeDtypeStruct((kv.shape[0], HEAD_DIM), F32)
+    gain = jax.ShapeDtypeStruct((1, gains.shape[1]), F32)
+    copied = by_rows + by_cols
+    specs = [rows(a) for a in by_rows] + [cols(a) for a in by_cols]
+    same = pl.BlockSpec(gain.shape, lambda i: (0, 0))
     return pl.pallas_call(
-        back_kernel,
-        grid=(nb, 2 * nq),
-        in_specs=[first(width), second(width), whole(seg), whole(gain), whole(w_q), whole(w_k), whole(w_v), whole(w_o),
-                  first(HEAD_DIM), pl.BlockSpec((1, seq, e3), lambda b, i: (b, 0, 0)), first(HEAD_DIM)] + thru,
-        out_specs=[second(width), const((width, HEAD_DIM)), const((width, 2 * HEAD_DIM)), const((HEAD_DIM, width))] + thru,
-        out_shape=[jax.ShapeDtypeStruct((nb, seq, width), BF), jax.ShapeDtypeStruct((width, HEAD_DIM), F32),
-                   jax.ShapeDtypeStruct((width, 2 * HEAD_DIM), F32),
-                   jax.ShapeDtypeStruct((HEAD_DIM, width), F32)] + [jax.ShapeDtypeStruct(c.shape, c.dtype) for c in carried],
-        scratch_shapes=[pltpu.VMEM((seq, e3), BF), pltpu.VMEM((seq, HEAD_DIM), F32), pltpu.VMEM((seq, HEAD_DIM), F32), pltpu.VMEM((width, e3), BF)],
-        name='back',
+        functools.partial(finish_kernel, len(copied)),
+        grid=(steps,),
+        in_specs=specs + [rows(kv), pl.BlockSpec(gains.shape, lambda i: (0, 0))],
+        out_specs=specs + [rows(half), rows(half), same, same],
+        out_shape=[jax.ShapeDtypeStruct(a.shape, a.dtype) for a in copied] + [half, half, gain, gain],
+        name='finish',
         compiler_params=pltpu.CompilerParams(vmem_limit_bytes=VMEM_LIMIT),
-        cost_estimate=pl.CostEstimate(flops=12_000_000_000, bytes_accessed=30_000_000, transcendentals=0),
-    )(dr, x, seg, gain, w_q, w_k, w_v, w_o, qkv, qkv, ctx, *carried)
+        cost_estimate=pl.CostEstimate(flops=1_000_000_000, bytes_accessed=60_000_000, transcendentals=0),
+    )(*copied, kv, gains)
 
 
 def mid_kernel(chips, part, x, dy, g_ref, wg, wu, wd, out, p_out, h_own, x_own, dres_own, gpart, dwg, dwu, dwd,
@@ -739,20 +798,22 @@
         own = tokens // tp_size
         g1 = gain_attn[None, :]
         g2 = gain_mlp[None, :]
-        weights = (w_q, w_k, w_v, w_o)
-
-        o_part, qkv, ctx = front_call(hidden, seg_ids, g1, *weights)
+        o_part, qkv, ctx = front_call(hidden, seg_ids, g1, w_q, w_k, w_v, w_o)
         dres, p_part, h_own, x_own, dres_own, g2_part, d_gate, d_up, d_down = mid_call(
             o_part.reshape(tokens, width), hidden, grad_out, g2, w_gate.T, w_up.T, w_down, chips, 1)
-        (y_out,) = ring_call(p_part, [h_own], [], AddTail, chips, 4)
-        ga_part, d_q, d_kv, d_o, y_out, d_gate, d_up, d_down = back_call(
-            dres.reshape(nb, seq, width), hidden, seg_ids, g1, *weights, qkv, ctx, (y_out, d_gate, d_up, d_down))
-        kv_rows = own // 2
-        kv_shape = (tp_size, 2, kv_rows, 2 * HEAD_DIM)
+        grad_q = jax.ShapeDtypeStruct((width, HEAD_DIM), F32)
+        grad_kv = jax.ShapeDtypeStruct((width, 2 * HEAD_DIM), F32)
+        grad_o = jax.ShapeDtypeStruct((HEAD_DIM, width), F32)
+        y_out, ga_part, d_q, d_kv, d_o = ring_call(
+            p_part, [h_own, dres.reshape(nb, seq, width), hidden, seg_ids, g1, w_q, w_k, w_v, w_o, qkv, ctx],
+            [jax.ShapeDtypeStruct((nb, seq, width), BF), grad_q, grad_kv, grad_o], AddTail, chips, 4,
+            task=back_task, in_any=(1, 2), out_any=(0,), extra=back_scratch(seq, width))
+        kv_shape = (tp_size, 2, own // 2, 2 * HEAD_DIM)
         dx, gains, d_kv = ring_call(ga_part.reshape(tokens, width), [x_own, dres_own, g1, g1, g2_part, d_kv.reshape(kv_shape)],
                                     [jax.ShapeDtypeStruct((2, width), F32), jax.ShapeDtypeStruct(kv_shape, F32)], AttnTail, chips, 3, True)
-        d_kv = d_kv.reshape(width, 2 * HEAD_DIM)
-        return (y_out.reshape(nb, seq, width), dx.reshape(nb, seq, width), gains[1], gains[0], d_q, d_kv[:, :HEAD_DIM], d_kv[:, HEAD_DIM:],
+        y_out, dx, d_q, d_gate, d_up, d_down, d_o, d_k, d_v, d_g2, d_g1 = finish_call(
+            [y_out, dx, d_q], [d_gate, d_up, d_down, d_o], d_kv.reshape(width, 2 * HEAD_DIM), gains)
+        return (y_out.reshape(nb, seq, width), dx.reshape(nb, seq, width), d_g1[0], d_g2[0], d_q, d_k, d_v,
                 d_o, d_gate.T, d_up.T, d_down)
 
     spec_act = P('data', None, None)

time: 464 us -> 443 us (0.955)
  local copies, waits for them, and re-layouts: 12.8 us -> 0 us
  Pallas kernels: 450 us -> 442 us
    pallas_call x1, Pallas kernels: 39.7 us -> 25.6 us  [finish_call(): pl.pallas_call(functools.partial(finish_kernel, len(copied)), grid=(steps...]
    unnamed x1 -> x0, local copies, waits for them, and re-layouts: 8.44 us -> none
    pallas_call x2, Pallas kernels: 201 us -> 207 us  [ring_call(): pl.pallas_call(body, out_shape=[jax.ShapeDtypeStruct(shape, BF)] + out_sh...]
where the time goes in v3:
time: 443 us
  Pallas kernels  442 us (100%)
    pallas_call x2, Pallas kernels, ring_call(): pl.pallas_call(body, out_shape=[jax.ShapeDtypeStruct(shape, BF)] + out_sh...  207 us
    pallas_call x1, Pallas kernels, mid_call(): pl.pallas_call(functools.partial(mid_kernel, chips), out_shape=[jax.Shape...  188 us
    pallas_call x1, Pallas kernels, finish_call(): pl.pallas_call(functools.partial(finish_kernel, len(copied)), grid=(steps...  25.6 us
    pallas_call x1, Pallas kernels, front_call(): pl.pallas_call(front_kernel, grid=(nb, seq // BLK), in_specs=[rowblk(widt...  20.8 us

profile of v3, /device:TPU:21, one launch (start us, length us, event | category | flops | bytes accessed | tf_op | source)
XLA Modules:
  0.0 442.8 jit_solution(8274388822364914146)
XLA Ops:
  0.6 20.8 %front.1 = (bf16[2,1024,2048]{2,1,0:T(8,128)(2,1)}, bf16[2,1024,384]{2,1,0:T(8,128)(2,1)}, bf16[2,1024,128]{2,1,0:T(8,128)(2,1)}) custom-call(bf16[2,1024,2048]{2,1,0:T(8,128)(2,1)} %refs_3_.1, s32[2,1024]{1,0:T(2,128)} %refs_4_.1, f32[1,2048]{1,0:T(1,128)} %bitcast.31, bf16[2048,128]{1,0:T(8,128)(2,1)} %refs_6_.1, bf16[2048,128]{1,0:T(8,128)(2,1)} %refs_7_.1, ...), custom_call_target="tpu_custom_call" | custom-call | flops 8000000000 | bytes 20000000 | tf_op jit(solution)/shard_map/front/pallas_call | solution.py:369
  21.4 188.3 %middle.1 = (bf16[16,2,4,16,2048]{4,3,2,1,0:T(8,128)(2,1)}, bf16[16,2,4,16,2048]{4,3,2,1,0:T(8,128)(2,1)}, bf16[2,4,16,2048]{3,2,1,0:T(8,128)(2,1)}, bf16[2,4,16...) custom-call(bf16[16,2,4,16,2048]{4,3,2,1,0:T(8,128)(2,1)} %bitcast.3, ...), custom_call_target="tpu_custom_call" | custom-call | flops 120000004096 | bytes 167772160 | tf_op jit(solution)/shard_map/middle/pallas_call | solution.py:773
  209.8 94.0 %ring_4.1 = (bf16[16,2,4,16,2048]{4,3,2,1,0:T(8,128)(2,1)}, bf16[2,1024,2048]{2,1,0:T(8,128)(2,1)}, f32[2048,128]{1,0:T(8,128)}, f32[2048,256]{1,0:T(8,128)}, f32[128,2048]{1,0:T(8,128)}) custom-call(bf16[16,2,4,16,2048]{4,3,2,1,0:T(8,128)(2,1)} %get-tuple-element.43.refs_0_, bf16[2,4,16,2048]{3,2,1,0:T(8,128)(2,1)} %get-tuple-element.44.refs_1_, ...), custom_call_target="tpu_custom_call" | custom-call | flops 80000000000 | bytes 16777216 | tf_op jit(solution)/shard_map/ring_4/pallas_call | solution.py:311
  303.8 113.2 %ring_3.1 = (bf16[16,2,4,16,2048]{4,3,2,1,0:T(8,128)(2,1)}, f32[2,2048]{1,0:T(2,128)}, f32[16,2,64,256]{3,2,1,0:T(8,128)}) custom-call(bf16[16,2,4,16,2048]{4,3,2,1,0:T(8,128)(2,1)} %bitcast.38, bf16[2,4,16,2048]{3,2,1,0:T(8,128)(2,1)} %get-tuple-element.50.refs_1_, f32[2,4,16,2048]{3,2,1,0:T(8,128)} %get-tuple-element.51.refs_2_, f32[1,2048]{1,0:T(1,128)} %bitcast.33, ...), custom_call_target="tpu_custom_call" | custom-call | flops 80000000000 | bytes 16777216 | tf_op jit(solution)/shard_map/ring_3/pallas_call | solution.py:311
  417.0 25.6 %finish.1 = (bf16[2048,2048]{1,0:T(8,128)(2,1)}, bf16[2048,2048]{1,0:T(8,128)(2,1)}, f32[2048,128]{1,0:T(8,128)}, f32[416,2048]{1,0:T(8,128)}, f32[416,2048]{1,0...) custom-call(bf16[2048,2048]{1,0:T(8,128)(2,1)} %bitcast.19, ...), custom_call_target="tpu_custom_call" | custom-call | flops 1000000000 | bytes 60000000 | tf_op jit(solution)/shard_map/finish/pallas_call | solution.py:498

commit v4 on v3

--- a/solution.py
+++ b/solution.py
@@ -145,13 +145,23 @@
 
     def work_share(n):
         if task:
-            span = 2 * (chips - 2)
-            pl.loop(n * work_count // span, (n + 1) * work_count // span)(work)
+            lead = chips
+            rest = work_count - lead
+            span = chips - 2
+            if isinstance(n, int):
+                work(jnp.int32(n))
+            else:
+                late = jnp.maximum(n - lead, 0)
+                lo = jnp.where(n < lead, n, lead + late * rest // span)
+                hi = jnp.where(n < lead, n + 1, lead + (late + 1) * rest // span)
+                pl.loop(lo, hi)(work)
+
+    work_share(0)
 
     @pl.loop(1, chips - 1)
     def _(s):
         rs_step(s, False)
-        work_share(s - 1)
+        work_share(s)
 
     def ag_copy(d, j, t, m):
         return pltpu.make_async_remote_copy(
@@ -176,6 +186,8 @@
             ag_copy(d, j, 0, chip).start()
             spread(d, j, chip)
     epilogue.end(outs, state)
+
+    work_share(chips - 1)
 
     if with_gain:
         for d in range(2):
@@ -216,7 +228,7 @@
     @pl.loop(1, chips - 1)
     def _(t):
         ag_step(t, False)
-        work_share(chips - 3 + t)
+        work_share(chips - 1 + t)
 
     ag_step(chips - 1, True)
     if task:
@@ -321,13 +333,17 @@
     return (res[0].reshape(tokens, width),) + tuple(res[1:])
 
 
-def masked_probs(q, k, seg_ref, b, row0):
-    n = q.shape[0]
-    seg_k = seg_ref[pl.ds(b, 1), :].astype(F32)
+def seg_column(seg_ref, b, row0, n):
     own = seg_ref[pl.ds(b, 1), pl.ds(row0, n)].astype(F32)
-    seg_q = jnp.transpose(jnp.broadcast_to(own, (128, n)))[:, :1]
+    return jnp.transpose(jnp.broadcast_to(own, (128, n)))[:, :1]
+
+
+def masked_probs(q, k, seg_q, seg_k, row0, split=0):
     s = mm_nt(q, k) * HEAD_DIM ** -0.5
-    rows = row0 + lax.broadcasted_iota(jnp.int32, s.shape, 0)
+    local = lax.broadcasted_iota(jnp.int32, s.shape, 0)
+    rows = row0 + local
+    if split:
+        rows = rows + jnp.where(local >= q.shape[0] // 2, split, 0)
     cols = lax.broadcasted_iota(jnp.int32, s.shape, 1)
     s = jnp.where((rows >= cols) & (seg_q == seg_k), s, -1e30)
     e = jnp.exp(s - jnp.max(s, axis=-1, keepdims=True))
@@ -339,49 +355,35 @@
         w_ref[:, n * HEAD_DIM:(n + 1) * HEAD_DIM] = ref[...]
 
 
-def front_kernel(x_ref, sg_ref, g_ref, wq_ref, wk_ref, wv_ref, wo_ref, o_ref, qkv_ref, ctx_ref, k_s, v_s, w_ref):
-    qi = pl.program_id(1)
-
-    @pl.when((qi == 0) & (pl.program_id(0) == 0))
+def front_kernel(x_ref, g_ref, wq_ref, wk_ref, wv_ref, qkv_ref, w_ref):
+    @pl.when(pl.program_id(0) == 0)
     def _():
-        k_s[...] = jnp.zeros_like(k_s)
-        v_s[...] = jnp.zeros_like(v_s)
         pack(w_ref, wq_ref, wk_ref, wv_ref)
 
-    normed, _ = rms_parts(x_ref[0])
-    a = (normed * g_ref[...]).astype(BF)
-    qkv = mm(a, w_ref[...]).astype(BF)
-    qkv_ref[0] = qkv
-    row0 = pl.multiple_of(qi * BLK, BLK)
-    k_s[pl.ds(row0, BLK)] = qkv[:, HEAD_DIM:2 * HEAD_DIM]
-    v_s[pl.ds(row0, BLK)] = qkv[:, 2 * HEAD_DIM:]
-    probs = masked_probs(qkv[:, :HEAD_DIM], k_s[...], sg_ref, pl.program_id(0), row0)
-    ctx = mm(probs.astype(BF), v_s[...]).astype(BF)
-    ctx_ref[0] = ctx
-    o_ref[0] = mm(ctx, wo_ref[...]).astype(BF)
-
-
-def front_call(x, seg, gain, w_q, w_k, w_v, w_o):
-    nb, seq, width = x.shape
+    normed, _ = rms_parts(x_ref[...])
+    qkv_ref[...] = mm((normed * g_ref[...]).astype(BF), w_ref[...]).astype(BF)
+
+
+def front_call(x, gain, w_q, w_k, w_v):
+    tokens, width = x.shape
     e3 = 3 * HEAD_DIM
-    rowblk = lambda n: pl.BlockSpec((1, BLK, n), lambda b, i: (b, i, 0))
-    whole = lambda arr: pl.BlockSpec(arr.shape, lambda b, i: (0, 0))
+    rowblk = lambda n: pl.BlockSpec((BLK, n), lambda i: (i, 0))
+    whole = lambda arr: pl.BlockSpec(arr.shape, lambda i: (0, 0))
     return pl.pallas_call(
         front_kernel,
-        grid=(nb, seq // BLK),
-        in_specs=[rowblk(width), whole(seg), whole(gain), whole(w_q), whole(w_k), whole(w_v), whole(w_o)],
-        out_specs=[rowblk(width), rowblk(e3), rowblk(HEAD_DIM)],
-        out_shape=[jax.ShapeDtypeStruct((nb, seq, width), BF), jax.ShapeDtypeStruct((nb, seq, e3), BF),
-                   jax.ShapeDtypeStruct((nb, seq, HEAD_DIM), BF)],
-        scratch_shapes=[pltpu.VMEM((seq, HEAD_DIM), BF), pltpu.VMEM((seq, HEAD_DIM), BF), pltpu.VMEM((width, e3), BF)],
+        grid=(tokens // BLK,),
+        in_specs=[rowblk(width), whole(gain), whole(w_q), whole(w_k), whole(w_v)],
+        out_specs=rowblk(e3),
+        out_shape=jax.ShapeDtypeStruct((tokens, e3), BF),
+        scratch_shapes=[pltpu.VMEM((width, e3), BF)],
         name='front',
         compiler_params=pltpu.CompilerParams(vmem_limit_bytes=VMEM_LIMIT),
-        cost_estimate=pl.CostEstimate(flops=8_000_000_000, bytes_accessed=20_000_000, transcendentals=0),
-    )(x, seg, gain, w_q, w_k, w_v, w_o)
+        cost_estimate=pl.CostEstimate(flops=4_000_000_000, bytes_accessed=12_000_000, transcendentals=0),
+    )(x, gain, w_q, w_k, w_v)
 
 
 def back_task(ins, outs, scratch):
-    dr_ref, x_ref, sg_ref, g_ref, wq_ref, wk_ref, wv_ref, wo_ref, qkv_ref, ctx_ref = ins[1:]
+    dr_ref, x_ref, sg_ref, g_ref, wq_ref, wk_ref, wv_ref, wo_ref, qkv_ref = ins[1:]
     ga_ref, dwq_ref, dkv_ref, dwo_ref = outs
     inb, gab, dqkv_s, dk_s, dv_s, w_ref, in_sem, ga_sem = scratch
     nb, seq, width = dr_ref.shape
@@ -430,14 +432,15 @@
         def _():
             dr = inb[n % 2]
             dctx = mm_nt(dr, wo_ref[...]).astype(BF)
-            dwo_ref[...] += mm_tn(ctx_ref[b, pl.ds(row0, BLK)], dr)
             q = qkv_ref[b, pl.ds(row0, BLK), :HEAD_DIM]
             k = qkv_ref[b, :, HEAD_DIM:2 * HEAD_DIM]
             v = qkv_ref[b, :, 2 * HEAD_DIM:]
-            probs = masked_probs(q, k, sg_ref, b, row0)
+            probs = masked_probs(q, k, seg_column(sg_ref, b, row0, BLK), sg_ref[pl.ds(b, 1), :].astype(F32), row0)
+            probs_b = probs.astype(BF)
+            dwo_ref[...] += mm_tn(mm(probs_b, v).astype(BF), dr)
             dp = mm_nt(dctx, v)
             ds = (probs * (dp - jnp.sum(dp * probs, axis=-1, keepdims=True)) * scale).astype(BF)
-            dv_s[...] += mm_tn(probs.astype(BF), dctx)
+            dv_s[...] += mm_tn(probs_b, dctx)
             dk_s[...] += mm_tn(ds, q)
             dqkv_s[pl.ds(row0, BLK), :HEAD_DIM] = mm(ds, k).astype(BF)
 
@@ -486,14 +489,18 @@
         outs[n_copy + 2 + n][...] = gains[n:n + 1, :]
 
 
-def finish_call(by_rows, by_cols, kv, gains):
+def finish_call(by_rows, by_parts, kv, gains):
     steps = 16
     rows = lambda a: pl.BlockSpec((a.shape[0] // steps, a.shape[1]), lambda i: (i, 0))
-    cols = lambda a: pl.BlockSpec((a.shape[0], a.shape[1] // steps), lambda i: (0, i))
+    def parts(a):
+        size = next(n for n in range(8, a.shape[0] + 1, 8) if a.shape[0] % n == 0 and a.shape[0] // n <= steps)
+        top = a.shape[0] // size - 1
+        return pl.BlockSpec((size, a.shape[1]), lambda i: (jnp.minimum(i, top), 0))
+
     half = jax.ShapeDtypeStruct((kv.shape[0], HEAD_DIM), F32)
     gain = jax.ShapeDtypeStruct((1, gains.shape[1]), F32)
-    copied = by_rows + by_cols
-    specs = [rows(a) for a in by_rows] + [cols(a) for a in by_cols]
+    copied = by_rows + by_parts
+    specs = [rows(a) for a in by_rows] + [parts(a) for a in by_parts]
     same = pl.BlockSpec(gain.shape, lambda i: (0, 0))
     return pl.pallas_call(
         functools.partial(finish_kernel, len(copied)),
@@ -507,9 +514,9 @@
     )(*copied, kv, gains)
 
 
-def mid_kernel(chips, part, x, dy, g_ref, wg, wu, wd, out, p_out, h_own, x_own, dres_own, gpart, dwg, dwu, dwd,
+def mid_kernel(chips, x, dy, g_ref, seg, qkv, wo, wg, wu, wd, out, p_out, h_own, x_own, dres_own, gpart, dwg, dwu, dwd,
                loc, oth, arr, gat, gat2, dyb, pst, gst, dy_own,
-               ld_sem, xs_sem, xr_sem, rs_sem, rr_sem, as_sem, ar_sem, ps_sem, pm_sem, own_sem, dy_sem, po_sem,
+               xs_sem, xr_sem, rs_sem, rr_sem, as_sem, ar_sem, ps_sem, pm_sem, own_sem, dy_sem, po_sem,
                xs2_sem, xr2_sem, rs2_sem, rr2_sem, as2_sem, ar2_sem, ps2_sem, pr2_sem, wo_sem):
     me = lax.axis_index('tp')
     chip = me // 2
@@ -531,22 +538,14 @@
     def chunk_at(d, s):
         return lax.rem(chip + (s if d == 1 else chips - s), chips)
 
-    def swap(d, s):
-        m = chunk_at(d, s)
-        return remote(part.at[m * 2 + 1 - core, d], oth.at[m, d], xs_sem, xr_sem.at[m, d], mate)
-
-    def load(d, s):
-        m = chunk_at(d, s)
-        return pltpu.make_async_copy(part.at[m * 2 + core, d], loc.at[m, d], ld_sem.at[m, d])
+    def swap(d, t):
+        m = chunk_at(d, t)
+        return remote(gst.at[t % 2, d, 1 - core], oth.at[m, d], xs_sem.at[t % 2, d], xr_sem.at[m, d], mate)
 
     def dy_copy(d, t):
         m = chunk_at(d, t)
         return pltpu.make_async_copy(dy.at[pl.ds(m * 2, 2), d], dyb.at[t % 2, d], dy_sem.at[t % 2, d])
 
-    for s in range(1, chips + 1):
-        for d in range(2):
-            swap(d, s % chips).start()
-            load(d, s % chips).start()
     x_load = pltpu.make_async_copy(x.at[me], x_own, own_sem.at[0])
     dy_load = pltpu.make_async_copy(dy.at[me], dy_own, own_sem.at[1])
     x_load.start()
@@ -559,25 +558,55 @@
     def rs_copy(d, j, s, m, ssem, rsem):
         return remote(loc.at[m, d, j], arr.at[s, d, j], ssem, rsem.at[s, d, j], nxt[d])
 
-    def rs_step(s, first):
-        for d in range(2):
-            load(d, s + 1).wait()
-            swap(d, s + 1).wait_recv()
+    own = SUB * ROWS
+    group = chips // qkv.shape[0]
+
+    def attend(t):
+        for d in range(2):
+            m = chunk_at(d, t)
+            b = m // group
+            base = pl.multiple_of((m % group) * 4 * own, 4 * own)
+            first = pl.multiple_of(base + d * own, own)
+            again = pl.multiple_of(base + (2 + d) * own, own)
+            q = jnp.concatenate([qkv[b, pl.ds(first, own), :HEAD_DIM], qkv[b, pl.ds(again, own), :HEAD_DIM]], axis=0)
+            col = seg_column(seg, b, base, 4 * own)
+            seg_q = jnp.concatenate([col[d * own:(d + 1) * own], col[(2 + d) * own:(3 + d) * own]], axis=0)
+            probs = masked_probs(q, qkv[b, :, HEAD_DIM:2 * HEAD_DIM], seg_q, seg[pl.ds(b, 1), :].astype(F32), first, own)
+            ctx = mm(probs.astype(BF), qkv[b, :, 2 * HEAD_DIM:]).astype(BF)
+            gst[t % 2, d] = mm(ctx, wo[...]).astype(BF).reshape(2, SUB, ROWS, width)
+            swap(d, t).start()
+
+    def rs_step(t, first):
+        for d in range(2):
+            swap(d, t).wait_recv()
         for j in range(SUB):
             for d in range(2):
-                m = chunk_at(d, s + 1)
-                v = loc[m, d, j].astype(F32) + oth[m, d, j].astype(F32)
+                m = chunk_at(d, t)
+                v = gst[t % 2, d, core, j].astype(F32) + oth[m, d, j].astype(F32)
                 if not first:
-                    rs_copy(d, j, s - 1, m, rs_sem, rr_sem).wait_recv()
-                    v = v + arr[s - 1, d, j].astype(F32)
+                    rs_copy(d, j, t - 2, m, rs_sem, rr_sem).wait_recv()
+                    v = v + arr[t - 2, d, j].astype(F32)
                 loc[m, d, j] = v.astype(BF)
-                rs_copy(d, j, s, m, rs_sem, rr_sem).start()
-
-    rs_step(0, True)
-
-    @pl.loop(1, last)
-    def _(s):
-        rs_step(s, False)
+                rs_copy(d, j, t - 1, m, rs_sem, rr_sem).start()
+
+    attend(jnp.int32(1))
+
+    @pl.loop(1, chips)
+    def _(t):
+        @pl.when(t > 1)
+        def _():
+            for d in range(2):
+                swap(d, t - 1).wait_send()
+
+        attend(t + 1)
+
+        @pl.when(t == 1)
+        def _():
+            rs_step(t, True)
+
+        @pl.when(t > 1)
+        def _():
+            rs_step(t, False)
 
     def ag_copy(d, j, t, m):
         return remote(gat.at[m * 2 + core, d, j], gat.at[m * 2 + core, d, j], as_sem, ar_sem.at[t, d, j], nxt[d])
@@ -588,12 +617,11 @@
     x_load.wait()
     dy_load.wait()
     for d in range(2):
-        load(d, 0).wait()
-        swap(d, 0).wait_recv()
+        swap(d, chips).wait_recv()
     for j in range(SUB):
         for d in range(2):
             rs_copy(d, j, last - 1, chip, rs_sem, rr_sem).wait_recv()
-            v = loc[chip, d, j].astype(F32) + oth[chip, d, j].astype(F32) + arr[last - 1, d, j].astype(F32)
+            v = gst[chips % 2, d, core, j].astype(F32) + oth[chip, d, j].astype(F32) + arr[last - 1, d, j].astype(F32)
             h = (x_own[d, j].astype(F32) + v.astype(BF).astype(F32)).astype(BF)
             h_own[d, j] = h
             normed, _ = rms_parts(h)
@@ -605,6 +633,9 @@
         return remote(ref, ref, sem, rsem, mate)
 
     bulk(arr, rs_sem, pr2_sem).wait_send()
+    for t in (chips - 1, chips):
+        for d in range(2):
+            swap(d, t).wait_send()
 
     def p_copy(d, t):
         m = chunk_at(d, t)
@@ -745,7 +776,7 @@
     ag2_step(last, False)
 
     bulk(gat2, ps2_sem, pr2_sem).wait_recv()
-    for sem in (xs_sem, ps_sem, ps2_sem):
+    for sem in (ps_sem, ps2_sem):
         bulk(oth, sem, pr2_sem).wait_send()
     for sem in (as_sem, rs2_sem, as2_sem):
         bulk(arr, sem, pr2_sem).wait_send()
@@ -756,8 +787,9 @@
     pltpu.make_async_copy(gat2, gat2, wo_sem).wait()
 
 
-def mid_call(part, x, dy, gain, w_gate, w_up, w_down, chips, cid):
-    tokens, width = part.shape
+def mid_call(x, dy, gain, seg, qkv, w_o, w_gate, w_up, w_down, chips, cid):
+    nb, seq, width = x.shape
+    tokens = nb * seq
     ff = w_down.shape[0]
     shape = (chips * 2, 2, SUB, ROWS, width)
     half = (chips, 2, SUB, ROWS, width)
@@ -775,16 +807,16 @@
         out_shape=[jax.ShapeDtypeStruct(shape, BF), jax.ShapeDtypeStruct(shape, BF), jax.ShapeDtypeStruct(piece, BF),
                    jax.ShapeDtypeStruct(piece, BF), jax.ShapeDtypeStruct(piece, F32), jax.ShapeDtypeStruct((1, width), F32),
                    grad, grad, grad],
-        in_specs=[anyspec] * 3 + [vm] * 4,
+        in_specs=[anyspec] * 2 + [vm] * 7,
         out_specs=[anyspec] * 2 + [vm] * 7,
         scratch_shapes=[
             vmb(half), vmb(half), vmb(arrive), vmb(shape), vmb(half), vmb(pair), vmb(pair), vmb(pair), vmb(piece),
-            dma((chips, 2)), dma, dma((chips, 2)), dma, steps, dma, steps, dma, dma((chips,)), dma((2,)), dma((2, 2)), dma((2, 2)),
+            dma((2, 2)), dma((chips, 2)), dma, steps, dma, steps, dma, dma((chips,)), dma((2,)), dma((2, 2)), dma((2, 2)),
             dma((2, 2)), dma((chips, 2)), dma, steps, dma, steps, dma, dma, dma],
         name='middle',
         compiler_params=pltpu.CompilerParams(collective_id=cid, has_side_effects=True, vmem_limit_bytes=67_000_000),
         cost_estimate=pl.CostEstimate(flops=120_000_000_000, bytes_accessed=40 * tokens * width, transcendentals=0),
-    )(part.reshape(shape), x.reshape(shape), dy.reshape(shape), gain, w_gate, w_up, w_down)
+    )(x.reshape(shape), dy.reshape(shape), gain, seg, qkv, w_o, w_gate, w_up, w_down)
     return (res[0].reshape(tokens, width), res[1].reshape(tokens, width)) + tuple(res[2:])
 
 
@@ -798,14 +830,14 @@
         own = tokens // tp_size
         g1 = gain_attn[None, :]
         g2 = gain_mlp[None, :]
-        o_part, qkv, ctx = front_call(hidden, seg_ids, g1, w_q, w_k, w_v, w_o)
+        qkv = front_call(hidden.reshape(tokens, width), g1, w_q, w_k, w_v).reshape(nb, seq, 3 * HEAD_DIM)
         dres, p_part, h_own, x_own, dres_own, g2_part, d_gate, d_up, d_down = mid_call(
-            o_part.reshape(tokens, width), hidden, grad_out, g2, w_gate.T, w_up.T, w_down, chips, 1)
+            hidden, grad_out, g2, seg_ids, qkv, w_o, w_gate.T, w_up.T, w_down, chips, 1)
         grad_q = jax.ShapeDtypeStruct((width, HEAD_DIM), F32)
         grad_kv = jax.ShapeDtypeStruct((width, 2 * HEAD_DIM), F32)
         grad_o = jax.ShapeDtypeStruct((HEAD_DIM, width), F32)
         y_out, ga_part, d_q, d_kv, d_o = ring_call(
-            p_part, [h_own, dres.reshape(nb, seq, width), hidden, seg_ids, g1, w_q, w_k, w_v, w_o, qkv, ctx],
+            p_part, [h_own, dres.reshape(nb, seq, width), hidden, seg_ids, g1, w_q, w_k, w_v, w_o, qkv],
             [jax.ShapeDtypeStruct((nb, seq, width), BF), grad_q, grad_kv, grad_o], AddTail, chips, 4,
             task=back_task, in_any=(1, 2), out_any=(0,), extra=back_scratch(seq, width))
         kv_shape = (tp_size, 2, own // 2, 2 * HEAD_DIM)

time: 443 us -> 438 us (0.989)
  Pallas kernels: 442 us -> 436 us
    pallas_call x1, Pallas kernels: 20.8 us -> 11.5 us  [front_call(): pl.pallas_call(front_kernel, grid=(tokens // BLK,), in_specs=[rowblk(widt...]
where the time goes in v4:
time: 438 us; the launch traced here: 437 us
  Pallas kernels  436 us (100%)
    pallas_call x2, Pallas kernels, ring_call(): pl.pallas_call(body, out_shape=[jax.ShapeDtypeStruct(shape, BF)] + out_sh...  206 us
    pallas_call x1, Pallas kernels, mid_call(): pl.pallas_call(functools.partial(mid_kernel, chips), out_shape=[jax.Shape...  192 us
    pallas_call x1, Pallas kernels, finish_call(): pl.pallas_call(functools.partial(finish_kernel, len(copied)), grid=(steps...  25.6 us
    pallas_call x1, Pallas kernels, front_call(): pl.pallas_call(front_kernel, grid=(tokens // BLK,), in_specs=[rowblk(widt...  11.5 us

profile of v4, /device:TPU:21, one launch (start us, length us, event | category | flops | bytes accessed | tf_op | source)
XLA Modules:
  0.0 436.8 jit_solution(2529353338227133151)
XLA Ops:
  0.6 11.5 %front.1 = bf16[2048,384]{1,0:T(8,128)(2,1)} custom-call(bf16[2048,2048]{1,0:T(8,128)(2,1)} %bitcast.24, f32[1,2048]{1,0:T(1,128)} %bitcast.33, bf16[2048,128]{1,0:T(8,128)(2,1)} %refs_6_.1, bf16[2048,128]{1,0:T(8,128)(2,1)} %refs_7_.1, bf16[2048,128]{1,0:T(8,128)(2,1)} %refs_8_.1), custom_call_target="tpu_custom_call" | custom-call | flops 4000000000 | bytes 12000000 | tf_op jit(solution)/shard_map/front/pallas_call | solution.py:372
  12.1 192.5 %middle.1 = (bf16[16,2,4,16,2048]{4,3,2,1,0:T(8,128)(2,1)}, bf16[16,2,4,16,2048]{4,3,2,1,0:T(8,128)(2,1)}, bf16[2,4,16,2048]{3,2,1,0:T(8,128)(2,1)}, bf16[2,4,16...) custom-call(bf16[16,2,4,16,2048]{4,3,2,1,0:T(8,128)(2,1)} %bitcast.2, ...), custom_call_target="tpu_custom_call" | custom-call | flops 120000004096 | bytes 167772160 | tf_op jit(solution)/shard_map/middle/pallas_call | solution.py:805
  204.6 93.2 %ring_4.1 = (bf16[16,2,4,16,2048]{4,3,2,1,0:T(8,128)(2,1)}, bf16[2,1024,2048]{2,1,0:T(8,128)(2,1)}, f32[2048,128]{1,0:T(8,128)}, f32[2048,256]{1,0:T(8,128)}, f32[128,2048]{1,0:T(8,128)}) custom-call(bf16[16,2,4,16,2048]{4,3,2,1,0:T(8,128)(2,1)} %get-tuple-element.39.refs_0_, bf16[2,4,16,2048]{3,2,1,0:T(8,128)(2,1)} %get-tuple-element.40.refs_1_, ...), custom_call_target="tpu_custom_call" | custom-call | flops 80000000000 | bytes 16777216 | tf_op jit(solution)/shard_map/ring_4/pallas_call | solution.py:323
  297.8 113.2 %ring_3.1 = (bf16[16,2,4,16,2048]{4,3,2,1,0:T(8,128)(2,1)}, f32[2,2048]{1,0:T(2,128)}, f32[16,2,64,256]{3,2,1,0:T(8,128)}) custom-call(bf16[16,2,4,16,2048]{4,3,2,1,0:T(8,128)(2,1)} %bitcast.40, bf16[2,4,16,2048]{3,2,1,0:T(8,128)(2,1)} %get-tuple-element.44.refs_1_, f32[2,4,16,2048]{3,2,1,0:T(8,128)} %get-tuple-element.45.refs_2_, f32[1,2048]{1,0:T(1,128)} %bitcast.35, ...), custom_call_target="tpu_custom_call" | custom-call | flops 80000000000 | bytes 16777216 | tf_op jit(solution)/shard_map/ring_3/pallas_call | solution.py:323
  411.0 25.6 %finish.1 = (bf16[2048,2048]{1,0:T(8,128)(2,1)}, bf16[2048,2048]{1,0:T(8,128)(2,1)}, f32[2048,128]{1,0:T(8,128)}, f32[416,2048]{1,0:T(8,128)}, f32[416,2048]{1,0...) custom-call(bf16[2048,2048]{1,0:T(8,128)(2,1)} %bitcast.20, ...), custom_call_target="tpu_custom_call" | custom-call | flops 1000000000 | bytes 60000000 | tf_op jit(solution)/shard_map/finish/pallas_call | solution.py:505

commit v5 on v4

--- a/solution.py
+++ b/solution.py
@@ -11,6 +11,7 @@
 SUB = 4
 ROWS = 16
 BLK = 256
+BOTH = (0, 1)
 BF = jnp.bfloat16
 F32 = jnp.float32
 MESH = pl.DeviceIdType.MESH
@@ -100,7 +101,7 @@
                 recv_sem=kpr, device_id=dev(mate), device_id_type=MESH).start()
 
     for s in range(1, chips + 1):
-        for d in range(2):
+        for d in BOTH:
             swap(d, s % chips).start()
             load(d, s % chips).start()
             if with_gain:
@@ -116,10 +117,10 @@
         swap(d, s).wait_recv()
 
     def rs_step(s, first):
-        for d in range(2):
+        for d in BOTH:
             ready(d, s + 1)
         for j in range(SUB):
-            for d in range(2):
+            for d in BOTH:
                 m = chunk_at(d, s + 1)
                 v = loc[m, d, j].astype(F32) + oth[m, d, j].astype(F32)
                 if not first:
@@ -128,7 +129,7 @@
                 loc[m, d, j] = v.astype(BF)
                 rs_copy(d, j, s, m).start()
         if with_gain:
-            for d in range(2):
+            for d in BOTH:
                 m = chunk_at(d, s + 1)
                 kswap(d, s + 1).wait_recv()
                 kv = kin[m * 2 + core, d] + koth[m, d]
@@ -145,16 +146,12 @@
 
     def work_share(n):
         if task:
-            lead = chips
-            rest = work_count - lead
-            span = chips - 2
+            lead = 2 * (2 * chips - 2) - work_count
             if isinstance(n, int):
                 work(jnp.int32(n))
             else:
-                late = jnp.maximum(n - lead, 0)
-                lo = jnp.where(n < lead, n, lead + late * rest // span)
-                hi = jnp.where(n < lead, n + 1, lead + (late + 1) * rest // span)
-                pl.loop(lo, hi)(work)
+                lo = jnp.where(n < lead, n, 2 * n - lead)
+                pl.loop(lo, lo + jnp.where(n < lead, 1, 2))(work)
 
     work_share(0)
 
@@ -174,11 +171,11 @@
             recv_sem=pr_sem, device_id=dev(mate), device_id_type=MESH).start()
         pltpu.make_async_copy(gat.at[m, d, j], out.at[m * 2 + core, d, j], wo_sem).start()
 
-    for d in range(2):
+    for d in BOTH:
         ready(d, 0)
     state = epilogue.begin(ins, outs)
     for j in range(SUB):
-        for d in range(2):
+        for d in BOTH:
             rs_copy(d, j, chips - 2, chip).wait_recv()
             v = loc[chip, d, j].astype(F32) + oth[chip, d, j].astype(F32) + arr[chips - 2, d, j].astype(F32)
             res, state = epilogue.piece(v.astype(BF).astype(F32), d, j, ins, outs, state)
@@ -190,7 +187,7 @@
     work_share(chips - 1)
 
     if with_gain:
-        for d in range(2):
+        for d in BOTH:
             kswap(d, 0).wait_recv()
             krs_copy(d, chips - 2, chip).wait_recv()
             kout[chip * 2 + core, d] = kin[chip * 2 + core, d] + koth[chip, d] + karr[chips - 2, d]
@@ -208,14 +205,14 @@
 
     def ag_step(t, last):
         for j in range(SUB):
-            for d in range(2):
+            for d in BOTH:
                 m = chunk_at(d, t)
                 ag_copy(d, j, t - 1, m).wait_recv()
                 if not last:
                     ag_copy(d, j, t, m).start()
                 spread(d, j, m)
         if with_gain:
-            for d in range(2):
+            for d in BOTH:
                 m = chunk_at(d, t)
                 kag_copy(d, t - 1, m).wait_recv()
                 if not last:
@@ -479,43 +476,55 @@
             pltpu.SemaphoreType.DMA((2,)), pltpu.SemaphoreType.DMA((2,))]
 
 
-def finish_kernel(n_copy, *refs):
-    ins, outs = refs[:n_copy + 2], refs[n_copy + 2:]
-    for n in range(n_copy):
-        outs[n][...] = ins[n][...]
-    kv, gains = ins[n_copy], ins[n_copy + 1]
-    for n in range(2):
-        outs[n_copy + n][...] = kv[:, n * HEAD_DIM:(n + 1) * HEAD_DIM]
-        outs[n_copy + 2 + n][...] = gains[n:n + 1, :]
-
-
-def finish_call(by_rows, by_parts, kv, gains):
-    steps = 16
-    rows = lambda a: pl.BlockSpec((a.shape[0] // steps, a.shape[1]), lambda i: (i, 0))
-    def parts(a):
-        size = next(n for n in range(8, a.shape[0] + 1, 8) if a.shape[0] % n == 0 and a.shape[0] // n <= steps)
-        top = a.shape[0] // size - 1
-        return pl.BlockSpec((size, a.shape[1]), lambda i: (jnp.minimum(i, top), 0))
-
+def finish_kernel(cuts, *refs):
+    n = len(cuts)
+    ins, kv, gains = refs[:n], refs[n], refs[n + 1]
+    outs, dk, dv, first, second = refs[n + 2:2 * n + 2], refs[2 * n + 2], refs[2 * n + 3], refs[2 * n + 4], refs[2 * n + 5]
+    bufs, kv_buf, rd_sem, wr_sem = refs[2 * n + 6:3 * n + 6], refs[3 * n + 6], refs[3 * n + 7], refs[3 * n + 8]
+    reads, writes = [], []
+    for src, dst, buf, parts in zip(ins, outs, bufs, cuts):
+        size = src.shape[0] // parts
+        for p in range(parts):
+            at = pl.ds(p * size, size)
+            reads.append(pltpu.make_async_copy(src.at[at], buf.at[at], rd_sem.at[len(reads)]))
+            writes.append([pltpu.make_async_copy(buf.at[at], dst.at[at], wr_sem.at[len(writes)])])
+    reads.append(pltpu.make_async_copy(kv, kv_buf, rd_sem.at[len(reads)]))
+    base = len(writes)
+    writes.append([pltpu.make_async_copy(kv_buf.at[:, pl.ds(k * HEAD_DIM, HEAD_DIM)], dst, wr_sem.at[base + k]) for k, dst in enumerate((dk, dv))])
+    for copy in reads:
+        copy.start()
+    first[...] = gains[0:1, :]
+    second[...] = gains[1:2, :]
+    for copy, group in zip(reads, writes):
+        copy.wait()
+        for put in group:
+            put.start()
+    for group in writes:
+        for put in group:
+            put.wait()
+
+
+def finish_call(copied, cuts, kv, gains):
     half = jax.ShapeDtypeStruct((kv.shape[0], HEAD_DIM), F32)
     gain = jax.ShapeDtypeStruct((1, gains.shape[1]), F32)
-    copied = by_rows + by_parts
-    specs = [rows(a) for a in by_rows] + [parts(a) for a in by_parts]
-    same = pl.BlockSpec(gain.shape, lambda i: (0, 0))
+    vm = pl.BlockSpec(memory_space=pltpu.VMEM)
+    anyspec = pl.BlockSpec(memory_space=pl.ANY)
+    n = len(copied)
+    dma = pltpu.SemaphoreType.DMA
     return pl.pallas_call(
-        functools.partial(finish_kernel, len(copied)),
-        grid=(steps,),
-        in_specs=specs + [rows(kv), pl.BlockSpec(gains.shape, lambda i: (0, 0))],
-        out_specs=specs + [rows(half), rows(half), same, same],
+        functools.partial(finish_kernel, cuts),
+        in_specs=[anyspec] * (n + 1) + [vm],
+        out_specs=[anyspec] * (n + 2) + [vm, vm],
         out_shape=[jax.ShapeDtypeStruct(a.shape, a.dtype) for a in copied] + [half, half, gain, gain],
+        scratch_shapes=[pltpu.VMEM(a.shape, a.dtype) for a in copied] + [pltpu.VMEM(kv.shape, F32), dma((sum(cuts) + 1,)), dma((sum(cuts) + 2,))],
         name='finish',
         compiler_params=pltpu.CompilerParams(vmem_limit_bytes=VMEM_LIMIT),
         cost_estimate=pl.CostEstimate(flops=1_000_000_000, bytes_accessed=60_000_000, transcendentals=0),
     )(*copied, kv, gains)
 
 
-def mid_kernel(chips, x, dy, g_ref, seg, qkv, wo, wg, wu, wd, out, p_out, h_own, x_own, dres_own, gpart, dwg, dwu, dwd,
-               loc, oth, arr, gat, gat2, dyb, pst, gst, dy_own,
+def mid_kernel(chips, x, dy, g_ref, seg, qkv, wo, wg_in, wu_in, wd_in, out, p_out, h_own, x_own, dres_own, gpart, dwg_out, dwu_out, dwd_out,
+               loc, oth, arr, gat, gat2, dyb, pst, gst, dy_own, wg, wu, wd, dwg, dwu, dwd, w_sem, dw_sem,
                xs_sem, xr_sem, rs_sem, rr_sem, as_sem, ar_sem, ps_sem, pm_sem, own_sem, dy_sem, po_sem,
                xs2_sem, xr2_sem, rs2_sem, rr2_sem, as2_sem, ar2_sem, ps2_sem, pr2_sem, wo_sem):
     me = lax.axis_index('tp')
@@ -546,11 +555,15 @@
         m = chunk_at(d, t)
         return pltpu.make_async_copy(dy.at[pl.ds(m * 2, 2), d], dyb.at[t % 2, d], dy_sem.at[t % 2, d])
 
+    weights = [pltpu.make_async_copy(src, dst, w_sem.at[n]) for n, (src, dst) in enumerate(((wg_in, wg), (wu_in, wu), (wd_in, wd)))]
+    grads = [pltpu.make_async_copy(src, dst, dw_sem.at[n]) for n, (src, dst) in enumerate(((dwg, dwg_out), (dwu, dwu_out), (dwd, dwd_out)))]
+    for copy in weights:
+        copy.start()
     x_load = pltpu.make_async_copy(x.at[me], x_own, own_sem.at[0])
     dy_load = pltpu.make_async_copy(dy.at[me], dy_own, own_sem.at[1])
     x_load.start()
     dy_load.start()
-    for d in range(2):
+    for d in BOTH:
         dy_copy(d, 0).start()
     for acc in (dwg, dwu, dwd):
         acc[...] = jnp.zeros_like(acc)
@@ -562,7 +575,7 @@
     group = chips // qkv.shape[0]
 
     def attend(t):
-        for d in range(2):
+        for d in BOTH:
             m = chunk_at(d, t)
             b = m // group
             base = pl.multiple_of((m % group) * 4 * own, 4 * own)
@@ -577,10 +590,10 @@
             swap(d, t).start()
 
     def rs_step(t, first):
-        for d in range(2):
+        for d in BOTH:
             swap(d, t).wait_recv()
         for j in range(SUB):
-            for d in range(2):
+            for d in BOTH:
                 m = chunk_at(d, t)
                 v = gst[t % 2, d, core, j].astype(F32) + oth[m, d, j].astype(F32)
                 if not first:
@@ -590,23 +603,15 @@
                 rs_copy(d, j, t - 1, m, rs_sem, rr_sem).start()
 
     attend(jnp.int32(1))
-
-    @pl.loop(1, chips)
+    rs_step(1, True)
+    attend(jnp.int32(2))
+
+    @pl.loop(2, chips)
     def _(t):
-        @pl.when(t > 1)
-        def _():
-            for d in range(2):
-                swap(d, t - 1).wait_send()
-
+        for d in BOTH:
+            swap(d, t - 1).wait_send()
         attend(t + 1)
-
-        @pl.when(t == 1)
-        def _():
-            rs_step(t, True)
-
-        @pl.when(t > 1)
-        def _():
-            rs_step(t, False)
+        rs_step(t, False)
 
     def ag_copy(d, j, t, m):
         return remote(gat.at[m * 2 + core, d, j], gat.at[m * 2 + core, d, j], as_sem, ar_sem.at[t, d, j], nxt[d])
@@ -616,10 +621,10 @@
 
     x_load.wait()
     dy_load.wait()
-    for d in range(2):
+    for d in BOTH:
         swap(d, chips).wait_recv()
     for j in range(SUB):
-        for d in range(2):
+        for d in BOTH:
             rs_copy(d, j, last - 1, chip, rs_sem, rr_sem).wait_recv()
             v = gst[chips % 2, d, core, j].astype(F32) + oth[chip, d, j].astype(F32) + arr[last - 1, d, j].astype(F32)
             h = (x_own[d, j].astype(F32) + v.astype(BF).astype(F32)).astype(BF)
@@ -634,7 +639,7 @@
 
     bulk(arr, rs_sem, pr2_sem).wait_send()
     for t in (chips - 1, chips):
-        for d in range(2):
+        for d in BOTH:
             swap(d, t).wait_send()
 
     def p_copy(d, t):
@@ -647,10 +652,10 @@
 
     def rs2_step(t, first):
         slot = t % 2
-        for d in range(2):
+        for d in BOTH:
             swap2(d, t).wait_recv()
         for j in range(SUB):
-            for d in range(2):
+            for d in BOTH:
                 m = chunk_at(d, t)
                 v = gst[slot, d, core, j].astype(F32) + oth[m, d, j].astype(F32)
                 if not first:
@@ -661,7 +666,7 @@
 
     def collect(t, onward):
         for j in range(SUB):
-            for d in range(2):
+            for d in BOTH:
                 m = chunk_at(d, t)
                 ag_copy(d, j, t - 1, m).wait_recv()
                 if onward:
@@ -669,6 +674,8 @@
                 spread(d, j, t, m)
 
     step = width // 4
+    for copy in weights:
+        copy.wait()
 
     @pl.loop(0, chips)
     def _(t):
@@ -686,16 +693,16 @@
 
         @pl.when(t < last)
         def _():
-            for d in range(2):
+            for d in BOTH:
                 dy_copy(d, t + 1).start()
 
         @pl.when(t >= 2)
         def _():
-            for d in range(2):
+            for d in BOTH:
                 p_copy(d, t - 2).wait()
                 swap2(d, t - 2).wait_send()
 
-        for d in range(2):
+        for d in BOTH:
             dy_copy(d, t).wait()
         bulk(gat.at[0], ps_sem, pm_sem.at[t]).wait_recv()
 
@@ -712,7 +719,7 @@
         for n in range(4):
             cs = slice(n * step, (n + 1) * step)
             gst[slot, :, :, :, :, cs] = (mm(dgate, wg[:, cs]) + mm(dupper, wu[:, cs])).astype(BF).reshape(2, 2, SUB, ROWS, step)
-        for d in range(2):
+        for d in BOTH:
             swap2(d, t).start()
         for n in range(4):
             cs = slice(n * step, (n + 1) * step)
@@ -720,12 +727,12 @@
             dwd[:, cs] += mm_tn(act, dyv[:, cs])
             dwg[:, cs] += mm_tn(dgate, mb[:, cs])
             dwu[:, cs] += mm_tn(dupper, mb[:, cs])
-        for d in range(2):
+        for d in BOTH:
             p_copy(d, t).start()
 
         @pl.when(t == 0)
         def _():
-            for d in range(2):
+            for d in BOTH:
                 loc[chip, d] = gst[0, d, core]
 
         @pl.when(t == 1)
@@ -735,6 +742,9 @@
         @pl.when(t > 1)
         def _():
             rs2_step(t, False)
+
+    for copy in grads:
+        copy.start()
 
     def ag2_copy(d, j, t, m):
         return remote(gat2.at[m, d, j], gat2.at[m, d, j], as2_sem, ar2_sem.at[t, d, j], nxt[d])
@@ -743,11 +753,11 @@
         remote(gat2.at[m, d, j], out.at[m * 2 + core, d, j], ps2_sem, pr2_sem, mate).start()
         pltpu.make_async_copy(gat2.at[m, d, j], out.at[m * 2 + core, d, j], wo_sem).start()
 
-    for d in range(2):
+    for d in BOTH:
         swap2(d, 0).wait_recv()
     total = jnp.zeros((1, width), F32)
     for j in range(SUB):
-        for d in range(2):
+        for d in BOTH:
             rs_copy(d, j, last - 1, chip, rs2_sem, rr2_sem).wait_recv()
             v = loc[chip, d, j].astype(F32) + oth[chip, d, j].astype(F32) + arr[last - 1, d, j].astype(F32)
             v = v.astype(BF).astype(F32)
@@ -762,7 +772,7 @@
 
     def ag2_step(t, onward):
         for j in range(SUB):
-            for d in range(2):
+            for d in BOTH:
                 m = chunk_at(d, t)
                 ag2_copy(d, j, t - 1, m).wait_recv()
                 if onward:
@@ -781,10 +791,12 @@
     for sem in (as_sem, rs2_sem, as2_sem):
         bulk(arr, sem, pr2_sem).wait_send()
     for t in (chips - 2, chips - 1):
-        for d in range(2):
+        for d in BOTH:
             p_copy(d, t).wait()
             swap2(d, t).wait_send()
     pltpu.make_async_copy(gat2, gat2, wo_sem).wait()
+    for copy in grads:
+        copy.wait()
 
 
 def mid_call(x, dy, gain, seg, qkv, w_o, w_gate, w_up, w_down, chips, cid):
@@ -802,15 +814,17 @@
     steps = dma((chips - 1, 2, SUB))
     vmb = lambda shp: pltpu.VMEM(shp, BF)
     grad = jax.ShapeDtypeStruct((ff, width), F32)
+    weight, acc = vmb((ff, width)), pltpu.VMEM((ff, width), F32)
     res = pl.pallas_call(
         functools.partial(mid_kernel, chips),
         out_shape=[jax.ShapeDtypeStruct(shape, BF), jax.ShapeDtypeStruct(shape, BF), jax.ShapeDtypeStruct(piece, BF),
                    jax.ShapeDtypeStruct(piece, BF), jax.ShapeDtypeStruct(piece, F32), jax.ShapeDtypeStruct((1, width), F32),
                    grad, grad, grad],
-        in_specs=[anyspec] * 2 + [vm] * 7,
-        out_specs=[anyspec] * 2 + [vm] * 7,
+        in_specs=[anyspec, anyspec] + [vm] * 4 + [anyspec] * 3,
+        out_specs=[anyspec, anyspec] + [vm] * 4 + [anyspec] * 3,
         scratch_shapes=[
             vmb(half), vmb(half), vmb(arrive), vmb(shape), vmb(half), vmb(pair), vmb(pair), vmb(pair), vmb(piece),
+            weight, weight, weight, acc, acc, acc, dma((3,)), dma((3,)),
             dma((2, 2)), dma((chips, 2)), dma, steps, dma, steps, dma, dma((chips,)), dma((2,)), dma((2, 2)), dma((2, 2)),
             dma((2, 2)), dma((chips, 2)), dma, steps, dma, steps, dma, dma, dma],
         name='middle',
@@ -844,7 +858,7 @@
         dx, gains, d_kv = ring_call(ga_part.reshape(tokens, width), [x_own, dres_own, g1, g1, g2_part, d_kv.reshape(kv_shape)],
                                     [jax.ShapeDtypeStruct((2, width), F32), jax.ShapeDtypeStruct(kv_shape, F32)], AttnTail, chips, 3, True)
         y_out, dx, d_q, d_gate, d_up, d_down, d_o, d_k, d_v, d_g2, d_g1 = finish_call(
-            [y_out, dx, d_q], [d_gate, d_up, d_down, d_o], d_kv.reshape(width, 2 * HEAD_DIM), gains)
+            [y_out, dx, d_q, d_gate, d_up, d_down, d_o], (4, 4, 1, 2, 2, 2, 1), d_kv.reshape(width, 2 * HEAD_DIM), gains)
         return (y_out.reshape(nb, seq, width), dx.reshape(nb, seq, width), d_g1[0], d_g2[0], d_q, d_k, d_v,
                 d_o, d_gate.T, d_up.T, d_down)
 

time: 438 us -> 428 us (0.977)
  Pallas kernels: 436 us -> 427 us
    pallas_call x1, Pallas kernels: 192 us -> 187 us  [mid_call(): pl.pallas_call(functools.partial(mid_kernel, chips), out_shape=[jax.Shape...]
where the time goes in v5:
time: 428 us; the launch traced here: 427 us
  Pallas kernels  427 us (100%)
    pallas_call x2, Pallas kernels, ring_call(): pl.pallas_call(body, out_shape=[jax.ShapeDtypeStruct(shape, BF)] + out_sh...  205 us
    pallas_call x1, Pallas kernels, mid_call(): pl.pallas_call(functools.partial(mid_kernel, chips), out_shape=[jax.Shape...  187 us
    pallas_call x1, Pallas kernels, finish_call(): pl.pallas_call(functools.partial(finish_kernel, cuts), in_specs=[anyspec]...  23.2 us
    pallas_call x1, Pallas kernels, front_call(): pl.pallas_call(front_kernel, grid=(tokens // BLK,), in_specs=[rowblk(widt...  11.5 us

profile of v5, /device:TPU:21, one launch (start us, length us, event | category | flops | bytes accessed | tf_op | source)
XLA Modules:
  0.0 427.5 jit_solution(17688499006088732778)
XLA Ops:
  0.6 11.5 %front.1 = bf16[2048,384]{1,0:T(8,128)(2,1)} custom-call(bf16[2048,2048]{1,0:T(8,128)(2,1)} %bitcast.24, f32[1,2048]{1,0:T(1,128)} %bitcast.33, bf16[2048,128]{1,0:T(8,128)(2,1)} %refs_6_.1, bf16[2048,128]{1,0:T(8,128)(2,1)} %refs_7_.1, bf16[2048,128]{1,0:T(8,128)(2,1)} %refs_8_.1), custom_call_target="tpu_custom_call" | custom-call | flops 4000000000 | bytes 12000000 | tf_op jit(solution)/shard_map/front/pallas_call | solution.py:369
  12.1 186.6 %middle.1 = (bf16[16,2,4,16,2048]{4,3,2,1,0:T(8,128)(2,1)}, bf16[16,2,4,16,2048]{4,3,2,1,0:T(8,128)(2,1)}, bf16[2,4,16,2048]{3,2,1,0:T(8,128)(2,1)}, bf16[2,4,16...) custom-call(bf16[16,2,4,16,2048]{4,3,2,1,0:T(8,128)(2,1)} %bitcast.2, ...), custom_call_target="tpu_custom_call" | custom-call | flops 120000004096 | bytes 167772160 | tf_op jit(solution)/shard_map/middle/pallas_call | solution.py:818
  198.7 92.1 %ring_4.1 = (bf16[16,2,4,16,2048]{4,3,2,1,0:T(8,128)(2,1)}, bf16[2,1024,2048]{2,1,0:T(8,128)(2,1)}, f32[2048,128]{1,0:T(8,128)}, f32[2048,256]{1,0:T(8,128)}, f32[128,2048]{1,0:T(8,128)}) custom-call(bf16[16,2,4,16,2048]{4,3,2,1,0:T(8,128)(2,1)} %get-tuple-element.39.refs_0_, bf16[2,4,16,2048]{3,2,1,0:T(8,128)(2,1)} %get-tuple-element.40.refs_1_, ...), custom_call_target="tpu_custom_call" | custom-call | flops 80000000000 | bytes 16777216 | tf_op jit(solution)/shard_map/ring_4/pallas_call | solution.py:320
  290.9 113.2 %ring_3.1 = (bf16[16,2,4,16,2048]{4,3,2,1,0:T(8,128)(2,1)}, f32[2,2048]{1,0:T(2,128)}, f32[16,2,64,256]{3,2,1,0:T(8,128)}) custom-call(bf16[16,2,4,16,2048]{4,3,2,1,0:T(8,128)(2,1)} %bitcast.40, bf16[2,4,16,2048]{3,2,1,0:T(8,128)(2,1)} %get-tuple-element.44.refs_1_, f32[2,4,16,2048]{3,2,1,0:T(8,128)} %get-tuple-element.45.refs_2_, f32[1,2048]{1,0:T(1,128)} %bitcast.35, ...), custom_call_target="tpu_custom_call" | custom-call | flops 80000000000 | bytes 16777216 | tf_op jit(solution)/shard_map/ring_3/pallas_call | solution.py:320
  404.1 23.2 %finish.1 = (bf16[2048,2048]{1,0:T(8,128)(2,1)}, bf16[2048,2048]{1,0:T(8,128)(2,1)}, f32[2048,128]{1,0:T(8,128)}, f32[416,2048]{1,0:T(8,128)}, f32[416,2048]{1,0...) custom-call(bf16[2048,2048]{1,0:T(8,128)(2,1)} %bitcast.20, ...), custom_call_target="tpu_custom_call" | custom-call | flops 1000000000 | bytes 60000000 | tf_op jit(solution)/shard_map/finish/pallas_call | solution.py:514
